TPU v7x, 32 devices: a whole 2x2x4 slice. The times are simulated.
32 devices in a mesh: sym: 4 (over y, x), row: 8 (over z, core).
Axes of the slice: x: 2, y: 2, z: 4, core: 2. Of those that a mesh axis runs over, the one named last changes fastest.
Arguments:
- inner_state: float32 [4, 6144, 128], P('sym', 'row'), may hold values from -6 to 6
- outer_state: float32 [4, 24, 128, 1024], P('sym', None, None, 'row'), may hold values from -6 to 6
- block_hamiltonian: bfloat16 [4, 6144, 6144], P('sym', 'row'), may hold values from -2 to 2, as said below
- dipole: bfloat16 [4, 6144, 6144], P('sym', 'row'), may hold values from -0.078125 to 0.078125
- field_strength: float32 [64], replicated, may hold values from -1.2 to 1.2
- dipole_links: int32 [3, 64], replicated, may hold values 0 or 1
- ghost_amplitude: float32 [4, 2, 6144], P('sym'), may hold values from -0.4 to 0.4
- surface_amplitude: float32 [4, 6144], P('sym'), may hold values from -3 to 3
- state_channel: int32 [4, 6144], P('sym'), may hold values from 0 to 23
- threshold: float32 [4, 24], P('sym'), may hold values from 0 to 1
Outputs:
- inner_next: float32 [4, 6144, 128], P('sym', 'row')
- outer_next: float32 [4, 24, 128, 1024], P('sym', None, None, 'row')
Inputs may be any that keep to these rules, and one draw needn't show every extreme that they name: `block_hamiltonian`: each block is a symmetric matrix.
All inputs are finite; a program needn't handle non-finite values.
Results may differ from a plain program's by a relative error of at most 0.0085.
Values may be sent and summed in bfloat16 or wider, within the bound.
No kernel may reach another device: no remote copies, remote signals or barrier semaphores. Data moves between devices by JAX's collectives and lax.ppermute only.
A program may use at most 128 MiB of HBM per device.

v0:
```python
import jax
import jax.numpy as jnp
from jax import lax
from jax.experimental import pallas as pl
from jax.experimental.pallas import tpu as pltpu
from jax.sharding import PartitionSpec as P


TERMS = 4
CORES = 2

time_step = 2.0
spacing = 1.5
radius_start = 20.0
charge = 1.0


BF16 = jnp.bfloat16
F32 = jnp.float32


def dot(a, b):
    return jnp.dot(a, b, preferred_element_type=F32)


def partner(i, by):
    return ((i // CORES) ^ by) * CORES + i % CORES


def chip_swap(x, by):
    total = lax.axis_size("row")
    return lax.ppermute(x, "row", [(i, partner(i, by)) for i in range(total)])


def core_swap(x):
    total = lax.axis_size("row")
    return lax.ppermute(x, "row", [(i, i ^ 1) for i in range(total)])


def to_block_below(x):
    count = lax.axis_size("sym")
    return lax.ppermute(x, "sym", [(i, i - 1) for i in range(1, count)])


def to_block_above(x):
    count = lax.axis_size("sym")
    return lax.ppermute(x, "sym", [(i, i + 1) for i in range(count - 1)])


def from_first_row(x):
    total = lax.axis_size("row")
    x = jnp.where(lax.axis_index("row") == 0, x, jnp.zeros_like(x))
    reach = 1
    while reach < total:
        pairs = [(i, i + reach) for i in range(reach) if i + reach < total]
        x = x + lax.ppermute(x, "row", pairs)
        reach *= 2
    return x


VMEM = pl.BlockSpec(memory_space=pltpu.VMEM)
SMEM = pl.BlockSpec(memory_space=pltpu.SMEM)


def local_call(kernel, out_shape, in_specs, operands, flops=0, scratch=()):
    return pl.pallas_call(
        kernel,
        in_specs=in_specs,
        out_specs=[VMEM] * len(out_shape),
        out_shape=out_shape,
        scratch_shapes=list(scratch),
        compiler_params=pltpu.CompilerParams(vmem_limit_bytes=7 * 2**20),
        cost_estimate=pl.CostEstimate(flops=flops, bytes_accessed=0, transcendentals=0),
    )(*operands)


def columns_of(index_ref, j, rows):
    return pl.ds(pl.multiple_of(index_ref[j] * rows, 128), rows)


def give_kernel(index_ref, d_ref, u_ref, out_ref, ut_ref):
    rows = u_ref.shape[0]
    ut_ref[...] = u_ref[...].astype(F32).T.astype(BF16)
    for k in range(out_ref.shape[0]):
        part = dot(ut_ref[...], d_ref[:, columns_of(index_ref, k, rows)])
        out_ref[k] = part.T.astype(BF16)


def lift_give(index, dipole_rows, u):
    rows, columns = u.shape
    chips = index.shape[0]
    return local_call(
        give_kernel,
        [
            jax.ShapeDtypeStruct((chips, rows, columns), BF16),
            jax.ShapeDtypeStruct((columns, rows), BF16),
        ],
        [SMEM, VMEM, VMEM],
        [index, dipole_rows, u],
        flops=2 * rows * rows * chips * columns,
    )


def keep_kernel(index_ref, d_ref, ut_ref, carry_ref, *rest):
    *outs, token = rest
    rows = ut_ref.shape[1]
    for k, out in enumerate(outs):
        part = dot(ut_ref[...], d_ref[:, columns_of(index_ref, k, rows)])
        out[...] = (part.T + carry_ref[k].astype(F32)).astype(BF16)
    token[...] = jnp.zeros_like(token)


def lift_keep(index, dipole_rows, ut, carry):
    columns, rows = ut.shape
    chips = index.shape[0]
    *lifted, token = local_call(
        keep_kernel,
        [jax.ShapeDtypeStruct((rows, columns), BF16)] * chips
        + [jax.ShapeDtypeStruct((8, 128), F32)],
        [SMEM, VMEM, VMEM, VMEM],
        [index, dipole_rows, ut, carry],
        flops=2 * rows * rows * chips * columns,
    )
    return lifted, token


def stack_kernel(token, *refs):
    *pieces_in, out = refs
    for k, ref in enumerate(pieces_in):
        out[k] = ref[...]


def stack(arrays, token):
    rows, columns = arrays[0].shape
    return local_call(
        stack_kernel,
        [jax.ShapeDtypeStruct((len(arrays), rows, columns), BF16)],
        [VMEM] * (1 + len(arrays)),
        [token, *arrays],
    )[0]


def assemble(index_ref, whole, refs):
    rows = refs[0].shape[0]
    j = 0
    for ref in refs:
        views = [ref] if len(ref.shape) == 2 else [ref.at[k] for k in range(ref.shape[0])]
        for view in views:
            whole[pl.ds(pl.multiple_of(index_ref[j] * rows, 128), rows), :] = view[...]
            j += 1


def row_dots(out, matrix, whole, finish):
    half = out.shape[0] // 2

    def step(i, carry):
        where = pl.ds(pl.multiple_of(i * half, 8), half)
        finish(where, dot(matrix[where, :], whole[...]))
        return carry

    lax.fori_loop(0, 2, step, 0)


def own_kernel(index_ref, h_ref, g_ref, *rest):
    *refs, y_ref, ghost_ref, whole = rest
    assemble(index_ref, whole, refs)

    def finish(where, product):
        y_ref[where, :] = product

    row_dots(y_ref, h_ref, whole, finish)
    ghosts = ghost_ref.shape[0]
    ghost = dot(g_ref[...], whole[...])
    ghost_ref[...] = ghost[:ghosts] + ghost[ghosts:]


def own_product(index, held, ghosts, refs):
    rows, columns = refs[0].shape
    states = held.shape[1]
    return local_call(
        own_kernel,
        [
            jax.ShapeDtypeStruct((rows, columns), F32),
            jax.ShapeDtypeStruct((ghosts.shape[0] // 2, columns), F32),
        ],
        [SMEM] + [VMEM] * (2 + len(refs)),
        [index, held, ghosts, *refs],
        flops=2 * held.shape[0] * states * columns,
        scratch=[pltpu.VMEM((states, columns), BF16)],
    )


def near_kernel(
    ghost_ref, near_ref, near_total_ref, potential_ref, sign_ref,
    slope_ref, near_out, near_total_out,
):
    channels = near_ref.shape[1]
    ghost_0, ghost_1 = ghost_ref[:channels], ghost_ref[channels:]
    slope = (near_ref[1] - ghost_0) * (1.0 / (2.0 * spacing))
    slope_ref[...] = jnp.zeros_like(slope_ref)
    for i in range(3):
        top = slope.astype(BF16)
        slope = slope - top.astype(F32)
        slope_ref[i * channels : (i + 1) * channels, :] = top
    count = near_ref.shape[0]
    points = [ghost_1, ghost_0] + [near_ref[i] for i in range(count)]
    half = ghost_0.shape[1] // 2
    for i in range(count - 2):
        laplace = (
            -points[i] + 16.0 * points[i + 1] - 30.0 * points[i + 2]
            + 16.0 * points[i + 3] - points[i + 4]
        ) * (1.0 / (12.0 * spacing * spacing))
        image = -0.5 * laplace + potential_ref[i] * points[i + 2]
        turned = pltpu.roll(image, half, 1) * sign_ref[0:1]
        near_out[i] = turned
        if i < near_total_ref.shape[0]:
            near_total_out[i] = near_total_ref[i] + turned


def near_step(ghost, near, near_total, potential, sign, depth):
    columns = near.shape[2]
    return local_call(
        near_kernel,
        [
            jax.ShapeDtypeStruct((depth, columns), BF16),
            jax.ShapeDtypeStruct((near.shape[0] - 2, *near.shape[1:]), F32),
            jax.ShapeDtypeStruct(near_total.shape, F32),
        ],
        [VMEM] * 5,
        [ghost, near, near_total, potential, sign],
    )


def settle_kernel(*refs):
    *terms, out = refs
    total = terms[0][...].astype(F32)
    for term in terms[1:]:
        total = total + term[...].astype(F32)
    out[...] = total.astype(BF16)


def settle(terms):
    return local_call(
        settle_kernel,
        [jax.ShapeDtypeStruct(terms[0].shape, BF16)],
        [VMEM] * len(terms),
        terms,
    )[0]


def upper_kernel(
    index_ref, d_ref, y_ref, hot_ref, slope_ref, surface_ref, vectors_ref, *rest
):
    *refs, out, whole = rest
    assemble(index_ref, whole, refs)

    def finish(where, product):
        source = dot(hot_ref[where, :], slope_ref[...])
        out[where, :] = (
            y_ref[where, :]
            + vectors_ref[0:1] * product
            + surface_ref[where, :] * source
        )

    row_dots(out, d_ref, whole, finish)


def upper_product(index, held, y, hot, slope, surface, vectors, refs):
    rows, columns = refs[0].shape
    states = held.shape[1]
    operands = [index, held, y, hot, slope, surface, vectors, *refs]
    return local_call(
        upper_kernel,
        [jax.ShapeDtypeStruct((rows, columns), F32)],
        [SMEM] + [VMEM] * (len(operands) - 1),
        operands,
        flops=2 * rows * states * columns,
        scratch=[pltpu.VMEM((states, columns), BF16)],
    )[0]


def close_kernel(image_ref, lower_ref, vectors_ref, total_ref, *outs):
    image = image_ref[...] + vectors_ref[1:2] * lower_ref[...].astype(F32)
    vec = pltpu.roll(image, image.shape[1] // 2, 1) * vectors_ref[2:3]
    outs[0][...] = total_ref[...] + vec
    if len(outs) > 1:
        outs[1][...] = vec.astype(BF16)


def close_order(image, lower, vectors, total, last):
    out_shape = [jax.ShapeDtypeStruct(image.shape, F32)]
    if not last:
        out_shape.append(jax.ShapeDtypeStruct(image.shape, BF16))
    return local_call(
        close_kernel, out_shape, [VMEM] * 4, [image, lower, vectors, total]
    )


def pieces(x, count):
    found = []
    for _ in range(count):
        top = lax.reduce_precision(x, 8, 7)
        found.append(top.astype(BF16))
        x = x - top
    return found


def rotate(values, factor):
    real_part, imag_part = jnp.split(values, 2, axis=-1)
    return jnp.concatenate([factor * imag_part, -factor * real_part], axis=-1)


def outer_step(w, potential):
    laplace = (-w[:-4] + 16.0 * w[1:-3] - 30.0 * w[2:-2] + 16.0 * w[3:-1] - w[4:]) / (
        12.0 * spacing * spacing
    )
    return -0.5 * laplace + potential * w[2:-2]


def per_device(
    inner_state,
    outer_state,
    block_hamiltonian,
    dipole,
    field_strength,
    dipole_links,
    ghost_amplitude,
    surface_amplitude,
    state_channel,
    threshold,
):
    hamiltonian_rows = block_hamiltonian[0]
    dipole_rows = dipole[0]
    rows, states = hamiltonian_rows.shape
    columns = inner_state.shape[2]
    channels = threshold.shape[1]
    radial_here = outer_state.shape[3]
    block_index = lax.axis_index("sym")
    row_index = lax.axis_index("row")
    row_count = lax.axis_size("row")
    chips = row_count // CORES
    chip, core = row_index // CORES, row_index % CORES
    margin = 2 * TERMS

    steps = jnp.arange(chips, dtype=jnp.int32)
    away = chip ^ steps
    give_index = away * CORES + 1 - core
    keep_index = away * CORES + core
    gather_index = jnp.concatenate([keep_index, give_index])

    link_float = dipole_links.astype(F32)
    link_zero = jnp.zeros((1, link_float.shape[1]), F32)
    link_table = jnp.concatenate([link_zero, link_float, link_zero], axis=0)
    link_pair = lax.dynamic_slice_in_dim(link_table, block_index, 2, 0)
    link_pair = jnp.concatenate([link_pair, link_pair], axis=1)
    column_field = jnp.concatenate([field_strength, field_strength])
    upper_factor = column_field * link_pair[1]
    lower_factor = column_field * link_pair[0]
    half_sign = jnp.where(jnp.arange(columns) < columns // 2, 1.0, -1.0).astype(F32)

    channel_ids = jnp.arange(channels, dtype=jnp.int32)
    all_hot = (channel_ids[:, None] == state_channel[0][None, :]).astype(F32)
    weighted = (ghost_amplitude[0][:, None, :] * all_hot[None]).reshape(2 * channels, states)
    ghost_matrix = jnp.concatenate(pieces(weighted, 2), axis=0)
    own_channel = lax.dynamic_slice_in_dim(state_channel[0], row_index * rows, rows, 0)
    own_surface = lax.dynamic_slice_in_dim(surface_amplitude[0], row_index * rows, rows, 0)
    depth = 128 * ((3 * channels + 127) // 128)
    slot = jnp.arange(depth, dtype=jnp.int32)
    own_hot = (
        (own_channel[:, None] == (slot % channels)[None, :]) & (slot < 3 * channels)[None, :]
    ).astype(BF16)
    half_surface = 0.5 * own_surface[:, None]

    outer0 = jnp.transpose(outer_state[0], (2, 0, 1))
    forward = [(i, i + 1) for i in range(row_count - 1)]
    backward = [(i + 1, i) for i in range(row_count - 1)]
    low = lax.ppermute(outer0[radial_here - margin :], "row", forward)
    high = lax.ppermute(outer0[:margin], "row", backward)
    near = from_first_row(outer0[: 2 * margin])

    def potential_at(points):
        radius = radius_start + spacing * points.astype(F32)
        return (threshold[0][None, :] - charge / radius[:, None])[:, :, None]

    near_potential = jnp.broadcast_to(
        potential_at(jnp.arange(2 * margin, dtype=jnp.int32)), near.shape
    )
    near_total = near[:margin]

    rounded = inner_state[0].astype(BF16)
    inner_total = inner_state[0]
    for order in range(1, TERMS + 1):
        factor = time_step / order
        sign = (factor * half_sign)[None]
        above = to_block_below(rounded)
        around = []
        for k in range(1, chips):
            around.append(chip_swap(rounded, k))
        rounded_other = core_swap(rounded)
        given, turned = lift_give(give_index, dipole_rows, rounded)
        carried = core_swap(given)
        lifted, token = lift_keep(keep_index, dipole_rows, turned, carried)
        landed = [lifted[0]]
        for k in reversed(range(1, chips)):
            landed.append(chip_swap(lifted[k], k))
        above_next = to_block_below(around[0])
        next_other = core_swap(around[0])
        own = stack(around[1:], token)
        above_own = to_block_below(own)
        own_other = core_swap(own)
        part, ghost = own_product(
            gather_index, hamiltonian_rows, ghost_matrix,
            [rounded, around[0], own, rounded_other, next_other, own_other],
        )
        slope, near, near_total = near_step(
            ghost, near, near_total, near_potential, sign, depth
        )
        vectors = jnp.stack([upper_factor, lower_factor, factor * half_sign])
        above_other = core_swap(above)
        next_above_other = core_swap(above_next)
        above_own_other = core_swap(above_own)
        settled = settle(landed)
        lower = to_block_above(settled)
        image = upper_product(
            gather_index, dipole_rows, part, own_hot, slope, half_surface, vectors,
            [above, above_next, above_own, above_other, next_above_other,
             above_own_other],
        )
        closed = close_order(image, lower, vectors, inner_total, order == TERMS)
        inner_total = closed[0]
        rounded = closed[-1]

    points = row_index * radial_here - margin + jnp.arange(
        radial_here + 2 * margin, dtype=jnp.int32
    )
    inside = (points < row_count * radial_here)[:, None, None]
    slab_potential = potential_at(points)
    w = jnp.concatenate([low, outer0, high], axis=0)
    outer_total = outer0
    for order in range(1, TERMS + 1):
        trim = slice(2 * order, points.shape[0] - 2 * order)
        w = rotate(outer_step(w, slab_potential[trim]), time_step / order)
        w = jnp.where(inside[trim], w, 0.0)
        extra = margin - 2 * order
        outer_total = outer_total + w[extra : extra + radial_here]
    first = jnp.where(row_index == 0, near_total, outer_total[:margin])
    outer_total = jnp.concatenate([first, outer_total[margin:]], axis=0)
    outer_total = jnp.transpose(outer_total, (1, 2, 0))
    return inner_total[None], outer_total[None]


def solution(mesh):
    return jax.shard_map(
        per_device,
        mesh=mesh,
        in_specs=(
            P("sym", "row", None),
            P("sym", None, None, "row"),
            P("sym", "row", None),
            P("sym", "row", None),
            P(),
            P(),
            P("sym", None, None),
            P("sym", None),
            P("sym", None),
            P("sym", None),
        ),
        out_specs=(P("sym", "row", None), P("sym", None, None, "row")),
        check_vma=False,
    )
```

profile of v0, /device:TPU:9, one launch (start us, length us, event | category | flops | bytes accessed | tf_op | source)
XLA Modules:
  0.0 294.2 jit_solution(5087611953226613080)
XLA Ops:
  5.3 3.7 %copy-done = bf16[1,768,6144]{2,1,0:T(8,128)(2,1)S(1)} copy-done((bf16[1,768,6144]{2,1,0:T(8,128)(2,1)S(1)}, bf16[1,768,6144]{2,1,0:T(8,128)(2,1)}, u32[]{:S(2)}) %copy-start) | copy-done | bytes 9437208
  26.0 3.7 %copy-done.1 = bf16[1,768,6144]{2,1,0:T(8,128)(2,1)S(1)} copy-done((bf16[1,768,6144]{2,1,0:T(8,128)(2,1)S(1)}, bf16[1,768,6144]{2,1,0:T(8,128)(2,1)}, u32[]{:S(2)}) %copy-start.1) | copy-done | bytes 9437208
  36.4 3.2 %collective-permute-done.8 = f32[16,24,128]{2,1,0:T(8,128)S(1)} collective-permute-done((f32[16,24,128]{2,1,0:T(8,128)S(1)}, f32[16,24,128]{2,1,0:T(8,128)S(1)}, u32[]{:S(2)}, u32[]{:S(2)}) %collective-permute-start.8) | collective-permute-done | bytes 196640 | tf_op jit(solution)/shard_map/ppermute | solution.py:56
  44.3 5.9 %collective-permute-done.11.rest_1_ = bf16[768,128]{1,0:T(8,128)(2,1)S(1)} collective-permute-done((bf16[768,128]{1,0:T(8,128)(2,1)S(1)}, bf16[768,128]{1,0:T(8,128)(2,1)S(1)}, u32[]{:S(2)}, u32[]{:S(2)}) %collective-permute-start.11) | collective-permute-done | bytes 196640 | tf_op jit(solution)/shard_map/ppermute | solution.py:42
  51.0 6.1 %collective-permute-done.9 = f32[16,24,128]{2,1,0:T(8,128)S(1)} collective-permute-done((f32[16,24,128]{2,1,0:T(8,128)S(1)}, f32[16,24,128]{2,1,0:T(8,128)S(1)}, u32[]{:S(2)}, u32[]{:S(2)}) %collective-permute-start.9) | collective-permute-done | bytes 196640 | tf_op jit(solution)/shard_map/ppermute | solution.py:56
  70.7 4.4 %collective-permute-start.19 = (bf16[768,128]{1,0:T(8,128)(2,1)S(1)}, bf16[768,128]{1,0:T(8,128)(2,1)S(1)}, u32[]{:S(2)}, u32[]{:S(2)}) collective-permute-start(bf16[768,128]{1,0:T(8,128)(2,1)S(1)} %shard_map.122), channel_id=1, source_target_pairs={{0,8},{8,16},{16,24},{1,9},{9,17},{17,25},{2,10},{10,18},{18,26},{... | collective-permute-start | bytes 589832 | tf_op jit(solution)/shard_map/ppermute | solution.py:47
  75.1 3.7 %copy-done.5 = bf16[1,768,6144]{2,1,0:T(8,128)(2,1)S(1)} copy-done((bf16[1,768,6144]{2,1,0:T(8,128)(2,1)S(1)}, bf16[1,768,6144]{2,1,0:T(8,128)(2,1)}, u32[]{:S(2)}) %copy-start.5) | copy-done | bytes 9437208
  78.8 3.9 %shard_map.119 = (f32[768,128]{1,0:T(8,128)S(1)}, f32[48,128]{1,0:T(8,128)S(1)}) custom-call(s32[8]{0:T(128)S(1)} %pad_add_fusion.index_ref, bf16[768,6144]{1,0:T(8,128)(2,1)S(1)} %bitcast.38, bf16[96,6144]{1,0:T(8,128)(2,1)S(1)} %pad_maximum_fusion.1.g_ref, bf16[768,128]{1,0:T(8,128)(2,1)S(1)} %bitcast_convert_fusion.u_ref.rest_0_, ...), custom_call_target="tpu_custom_call" | custom-call | flops 1207959552 | tf_op jit(solution)/shard_map/pallas_call | solution.py:66
  83.7 3.7 %copy-done.2 = bf16[1,768,6144]{2,1,0:T(8,128)(2,1)S(1)} copy-done((bf16[1,768,6144]{2,1,0:T(8,128)(2,1)S(1)}, bf16[1,768,6144]{2,1,0:T(8,128)(2,1)}, u32[]{:S(2)}) %copy-start.2) | copy-done | bytes 9437208
  87.4 3.5 %shard_map.121.image_ref = f32[768,128]{1,0:T(8,128)S(1)} custom-call(s32[8]{0:T(128)S(1)} %pad_add_fusion.index_ref, bf16[768,6144]{1,0:T(8,128)(2,1)S(1)} %bitcast.24, f32[768,128]{1,0:T(8,128)S(1)} %get-tuple-element.58.y_ref, bf16[768,128]{1,0:T(8,128)(2,1)S(1)} %and_convert_fusion.hot_ref, bf16[128,128]{1,0:T(8,128)(2,1)S(1)} %get-tuple-element.60.slope_ref, ...), custom_call_target="tpu_custom_call" | custom-call | flops 1207959552 | tf_op jit(solution)/shard_map/pallas_call | solution.py:66
  95.0 4.8 %collective-permute-start.22 = (bf16[768,128]{1,0:T(8,128)(2,1)S(1)}, bf16[768,128]{1,0:T(8,128)(2,1)S(1)}, u32[]{:S(2)}, u32[]{:S(2)}) collective-permute-start(bf16[768,128]{1,0:T(8,128)(2,1)S(1)} %get-tuple-element.65.u_ref.rest_0_), channel_id=1, source_target_pairs={{0,4},{1,5},{2,6},{3,7},{4,0},{5,1},{6,2},{7,3},{8,12},{9,13},{10,... | collective-permute-start | bytes 589832 | tf_op jit(solution)/shard_map/ppermute | solution.py:32
  102.6 3.3 %collective-permute-start.71 = (f32[8,24,128]{2,1,0:T(8,128)}, f32[8,24,128]{2,1,0:T(8,128)}, u32[]{:S(2)}, u32[]{:S(2)}) collective-permute-start(f32[8,24,128]{2,1,0:T(8,128)} %get-tuple-element.120), channel_id=1, source_target_pairs={{0,1},{1,2},{2,3},{3,4},{4,5},{5,6},{6,7},{8,9},{9,10},{10,11},{11... | collective-permute-start | bytes 294920 | tf_op jit(solution)/shard_map/ppermute | solution.py:377
  107.9 3.7 %copy-done.3 = bf16[1,768,6144]{2,1,0:T(8,128)(2,1)S(1)} copy-done((bf16[1,768,6144]{2,1,0:T(8,128)(2,1)S(1)}, bf16[1,768,6144]{2,1,0:T(8,128)(2,1)}, u32[]{:S(2)}) %copy-start.3) | copy-done | bytes 9437208
  125.3 3.4 %collective-permute-done.28.rest_1_ = bf16[768,128]{1,0:T(8,128)(2,1)S(1)} collective-permute-done((bf16[768,128]{1,0:T(8,128)(2,1)}, bf16[768,128]{1,0:T(8,128)(2,1)S(1)}, u32[]{:S(2)}, u32[]{:S(2)}) %collective-permute-start.28) | collective-permute-done | bytes 196640 | tf_op jit(solution)/shard_map/ppermute | solution.py:42
  131.8 5.1 %collective-permute-done.33.refs_1_ = bf16[768,128]{1,0:T(8,128)(2,1)S(1)} collective-permute-done((bf16[768,128]{1,0:T(8,128)(2,1)S(1)}, bf16[768,128]{1,0:T(8,128)(2,1)S(1)}, u32[]{:S(2)}, u32[]{:S(2)}) %collective-permute-start.33) | collective-permute-done | bytes 196640 | tf_op jit(solution)/shard_map/ppermute | solution.py:32
  137.5 3.4 %collective-permute-done.34.refs_2_ = bf16[768,128]{1,0:T(8,128)(2,1)S(1)} collective-permute-done((bf16[768,128]{1,0:T(8,128)(2,1)S(1)}, bf16[768,128]{1,0:T(8,128)(2,1)S(1)}, u32[]{:S(2)}, u32[]{:S(2)}) %collective-permute-start.34) | collective-permute-done | bytes 196640 | tf_op jit(solution)/shard_map/ppermute | solution.py:32
  143.3 5.9 %collective-permute-start.36 = (bf16[768,128]{1,0:T(8,128)(2,1)S(1)}, bf16[768,128]{1,0:T(8,128)(2,1)S(1)}, u32[]{:S(2)}, u32[]{:S(2)}) collective-permute-start(bf16[768,128]{1,0:T(8,128)(2,1)S(1)} %shard_map.130), channel_id=1, source_target_pairs={{0,8},{8,16},{16,24},{1,9},{9,17},{17,25},{2,10},{10,18},{18,26},{... | collective-permute-start | bytes 589832 | tf_op jit(solution)/shard_map/ppermute | solution.py:47
  149.3 4.3 %shard_map.127 = (f32[768,128]{1,0:T(8,128)S(1)}, f32[48,128]{1,0:T(8,128)S(1)}) custom-call(s32[8]{0:T(128)S(1)} %pad_add_fusion.index_ref, bf16[768,6144]{1,0:T(8,128)(2,1)S(1)} %bitcast.41, bf16[96,6144]{1,0:T(8,128)(2,1)S(1)} %pad_maximum_fusion.1.g_ref, bf16[768,128]{1,0:T(8,128)(2,1)S(1)} %get-tuple-element.65.u_ref.rest_0_, ...), custom_call_target="tpu_custom_call" | custom-call | flops 1207959552 | tf_op jit(solution)/shard_map/pallas_call | solution.py:66
  153.8 3.5 %shard_map.129.image_ref = f32[768,128]{1,0:T(8,128)S(1)} custom-call(s32[8]{0:T(128)S(1)} %pad_add_fusion.index_ref, bf16[768,6144]{1,0:T(8,128)(2,1)S(1)} %bitcast.31, f32[768,128]{1,0:T(8,128)S(1)} %get-tuple-element.69.y_ref, bf16[768,128]{1,0:T(8,128)(2,1)S(1)} %and_convert_fusion.hot_ref, bf16[128,128]{1,0:T(8,128)(2,1)S(1)} %get-tuple-element.73.slope_ref, ...), custom_call_target="tpu_custom_call" | custom-call | flops 1207959552 | tf_op jit(solution)/shard_map/pallas_call | solution.py:66
  167.0 9.1 %collective-permute-done.37.rest_1_ = bf16[768,128]{1,0:T(8,128)(2,1)S(1)} collective-permute-done((bf16[768,128]{1,0:T(8,128)(2,1)S(1)}, bf16[768,128]{1,0:T(8,128)(2,1)S(1)}, u32[]{:S(2)}, u32[]{:S(2)}) %collective-permute-start.37) | collective-permute-done | bytes 196640 | tf_op jit(solution)/shard_map/ppermute | solution.py:32
  184.9 3.5 %collective-permute-start.51 = (bf16[768,128]{1,0:T(8,128)(2,1)S(1)}, bf16[768,128]{1,0:T(8,128)(2,1)S(1)}, u32[]{:S(2)}, u32[]{:S(2)}) collective-permute-start(bf16[768,128]{1,0:T(8,128)(2,1)S(1)} %get-tuple-element.90), channel_id=1, source_target_pairs={{0,4},{1,5},{2,6},{3,7},{4,0},{5,1},{6,2},{7,3},{8,12},{9,13},{10,... | collective-permute-start | bytes 589832 | tf_op jit(solution)/shard_map/ppermute | solution.py:32
  191.7 7.2 %collective-permute-done.50.refs_1_ = bf16[768,128]{1,0:T(8,128)(2,1)S(1)} collective-permute-done((bf16[768,128]{1,0:T(8,128)(2,1)S(1)}, bf16[768,128]{1,0:T(8,128)(2,1)S(1)}, u32[]{:S(2)}, u32[]{:S(2)}) %collective-permute-start.50) | collective-permute-done | bytes 196640 | tf_op jit(solution)/shard_map/ppermute | solution.py:32
  204.4 6.4 %collective-permute-start.53 = (bf16[768,128]{1,0:T(8,128)(2,1)S(1)}, bf16[768,128]{1,0:T(8,128)(2,1)S(1)}, u32[]{:S(2)}, u32[]{:S(2)}) collective-permute-start(bf16[768,128]{1,0:T(8,128)(2,1)S(1)} %shard_map.138), channel_id=1, source_target_pairs={{0,8},{8,16},{16,24},{1,9},{9,17},{17,25},{2,10},{10,18},{18,26},{... | collective-permute-start | bytes 589832 | tf_op jit(solution)/shard_map/ppermute | solution.py:47
  210.8 3.9 %shard_map.135 = (f32[768,128]{1,0:T(8,128)S(1)}, f32[48,128]{1,0:T(8,128)S(1)}) custom-call(s32[8]{0:T(128)S(1)} %pad_add_fusion.index_ref, bf16[768,6144]{1,0:T(8,128)(2,1)S(1)} %bitcast.42, bf16[96,6144]{1,0:T(8,128)(2,1)S(1)} %pad_maximum_fusion.1.g_ref, bf16[768,128]{1,0:T(8,128)(2,1)S(1)} %get-tuple-element.79.u_ref.rest_0_, ...), custom_call_target="tpu_custom_call" | custom-call | flops 1207959552 | tf_op jit(solution)/shard_map/pallas_call | solution.py:66
  214.9 3.5 %shard_map.137.image_ref = f32[768,128]{1,0:T(8,128)S(1)} custom-call(s32[8]{0:T(128)S(1)} %pad_add_fusion.index_ref, bf16[768,6144]{1,0:T(8,128)(2,1)S(1)} %bitcast.34, f32[768,128]{1,0:T(8,128)S(1)} %get-tuple-element.83.y_ref, bf16[768,128]{1,0:T(8,128)(2,1)S(1)} %and_convert_fusion.hot_ref, bf16[128,128]{1,0:T(8,128)(2,1)S(1)} %get-tuple-element.87.slope_ref, ...), custom_call_target="tpu_custom_call" | custom-call | flops 1207959552 | tf_op jit(solution)/shard_map/pallas_call | solution.py:66
  230.0 7.2 %collective-permute-done.56.refs_0_ = bf16[768,128]{1,0:T(8,128)(2,1)S(1)} collective-permute-done((bf16[768,128]{1,0:T(8,128)(2,1)S(1)}, bf16[768,128]{1,0:T(8,128)(2,1)S(1)}, u32[]{:S(2)}, u32[]{:S(2)}) %collective-permute-start.56) | collective-permute-done | bytes 196640 | tf_op jit(solution)/shard_map/ppermute | solution.py:32
  237.2 3.4 %collective-permute-start.68 = (bf16[768,128]{1,0:T(8,128)(2,1)S(1)}, bf16[768,128]{1,0:T(8,128)(2,1)S(1)}, u32[]{:S(2)}, u32[]{:S(2)}) collective-permute-start(bf16[768,128]{1,0:T(8,128)(2,1)S(1)} %get-tuple-element.104), channel_id=1, source_target_pairs={{0,4},{1,5},{2,6},{3,7},{4,0},{5,1},{6,2},{7,3},{8,12},{9,13},{10,... | collective-permute-start | bytes 589832 | tf_op jit(solution)/shard_map/ppermute | solution.py:32
  240.6 10.8 %collective-permute-done.57.refs_1_ = bf16[768,128]{1,0:T(8,128)(2,1)S(1)} collective-permute-done((bf16[768,128]{1,0:T(8,128)(2,1)S(1)}, bf16[768,128]{1,0:T(8,128)(2,1)S(1)}, u32[]{:S(2)}, u32[]{:S(2)}) %collective-permute-start.57) | collective-permute-done | bytes 196640 | tf_op jit(solution)/shard_map/ppermute | solution.py:32
  267.2 4.9 %collective-permute-start.70 = (bf16[768,128]{1,0:T(8,128)(2,1)}, bf16[768,128]{1,0:T(8,128)(2,1)}, u32[]{:S(2)}, u32[]{:S(2)}) collective-permute-start(bf16[768,128]{1,0:T(8,128)(2,1)} %shard_map.146), channel_id=1, source_target_pairs={{0,8},{8,16},{16,24},{1,9},{9,17},{17,25},{2,10},{10,18},{18,26},{... | collective-permute-start | bytes 589832 | tf_op jit(solution)/shard_map/ppermute | solution.py:47
  275.6 3.9 %shard_map.143 = (f32[768,128]{1,0:T(8,128)S(1)}, f32[48,128]{1,0:T(8,128)S(1)}) custom-call(s32[8]{0:T(128)S(1)} %pad_add_fusion.index_ref, bf16[768,6144]{1,0:T(8,128)(2,1)S(1)} %bitcast.43, bf16[96,6144]{1,0:T(8,128)(2,1)S(1)} %pad_maximum_fusion.1.g_ref, bf16[768,128]{1,0:T(8,128)(2,1)S(1)} %get-tuple-element.93.u_ref.rest_0_, ...), custom_call_target="tpu_custom_call" | custom-call | flops 1207959552 | tf_op jit(solution)/shard_map/pallas_call | solution.py:66
  284.5 3.7 %copy-done.4 = bf16[1,768,6144]{2,1,0:T(8,128)(2,1)S(1)} copy-done((bf16[1,768,6144]{2,1,0:T(8,128)(2,1)S(1)}, bf16[1,768,6144]{2,1,0:T(8,128)(2,1)}, u32[]{:S(2)}) %copy-start.4) | copy-done | bytes 9437208
  288.2 4.2 %shard_map.145.image_ref = f32[768,128]{1,0:T(8,128)S(1)} custom-call(s32[8]{0:T(128)S(1)} %pad_add_fusion.index_ref, bf16[768,6144]{1,0:T(8,128)(2,1)S(1)} %bitcast.37, f32[768,128]{1,0:T(8,128)S(1)} %get-tuple-element.97.y_ref, bf16[768,128]{1,0:T(8,128)(2,1)S(1)} %and_convert_fusion.hot_ref, bf16[128,128]{1,0:T(8,128)(2,1)S(1)} %get-tuple-element.101.slope_ref, ...), custom_call_target="tpu_custom_call" | custom-call | flops 1207959552 | tf_op jit(solution)/shard_map/pallas_call | solution.py:66
  (319 shorter events, 141.7 us)
Async XLA Ops:
  1.7 30.2 %collective-permute-start.2 = (bf16[768,128]{1,0:T(8,128)(2,1)S(1)}, bf16[768,128]{1,0:T(8,128)(2,1)S(1)}, u32[]{:S(2)}, u32[]{:S(2)}) collective-permute-start(bf16[768,128]{1,0:T(8,128)(2,1)S(1)} %bitcast_convert_fusion.u_ref.rest_0_), channel_id=1, source_target_pairs={{0,4},{1,5},{2,6},{3,7},{4,0},{5,1},{6,2},{7,3},{8,12},{9,13},{10,... | collective-permute-start | bytes 589832 | tf_op jit(solution)/shard_map/ppermute | solution.py:32
  4.0 29.1 %collective-permute-start.3 = (bf16[768,128]{1,0:T(8,128)(2,1)S(1)}, bf16[768,128]{1,0:T(8,128)(2,1)S(1)}, u32[]{:S(2)}, u32[]{:S(2)}) collective-permute-start(bf16[768,128]{1,0:T(8,128)(2,1)S(1)} %bitcast_convert_fusion.u_ref.rest_0_), channel_id=1, source_target_pairs={{0,6},{1,7},{2,4},{3,5},{4,2},{5,3},{6,0},{7,1},{8,14},{9,15},{10,... | collective-permute-start | bytes 589832 | tf_op jit(solution)/shard_map/ppermute | solution.py:32
  4.0 31.1 %collective-permute-start = (bf16[768,128]{1,0:T(8,128)(2,1)S(1)}, bf16[768,128]{1,0:T(8,128)(2,1)S(1)}, u32[]{:S(2)}, u32[]{:S(2)}) collective-permute-start(bf16[768,128]{1,0:T(8,128)(2,1)S(1)} %bitcast_convert_fusion.u_ref.rest_0_), channel_id=1, source_target_pairs={{0,2},{1,3},{2,0},{3,1},{4,6},{5,7},{6,4},{7,5},{8,10},{9,11},{10,... | collective-permute-start | bytes 589832 | tf_op jit(solution)/shard_map/ppermute | solution.py:32
  23.6 18.1 %collective-permute-start.4 = (bf16[768,128]{1,0:T(8,128)(2,1)S(1)}, bf16[768,128]{1,0:T(8,128)(2,1)S(1)}, u32[]{:S(2)}, u32[]{:S(2)}) collective-permute-start(bf16[768,128]{1,0:T(8,128)(2,1)S(1)} %bitcast_convert_fusion.u_ref.rest_0_), channel_id=1, source_target_pairs={{0,1},{1,0},{2,3},{3,2},{4,5},{5,4},{6,7},{7,6},{8,9},{9,8},{10,11... | collective-permute-start | bytes 589832 | tf_op jit(solution)/shard_map/ppermute | solution.py:37
  24.7 19.1 %collective-permute-start.10 = (bf16[768,128]{1,0:T(8,128)(2,1)S(1)}, bf16[768,128]{1,0:T(8,128)(2,1)S(1)}, u32[]{:S(2)}, u32[]{:S(2)}) collective-permute-start(bf16[768,128]{1,0:T(8,128)(2,1)S(1)} %bitcast_convert_fusion.u_ref.rest_0_), channel_id=1, source_target_pairs={{8,0},{16,8},{24,16},{9,1},{17,9},{25,17},{10,2},{18,10},{26,18},{... | collective-permute-start | bytes 589832 | tf_op jit(solution)/shard_map/ppermute | solution.py:42
  33.2 23.9 %collective-permute-start.12 = (bf16[2,768,128]{2,1,0:T(8,128)(2,1)S(1)}, bf16[2,768,128]{2,1,0:T(8,128)(2,1)S(1)}, u32[]{:S(2)}, u32[]{:S(2)}) collective-permute-start(bf16[2,768,128]{2,1,0:T(8,128)(2,1)S(1)} %shard_map.118.rest_2_), channel_id=1, source_target_pairs={{8,0},{16,8},{24,16},{9,1},{17,9},{25,17},{10,2},{18,10},{26,18},{... | collective-permute-start | bytes 1179656 | tf_op jit(solution)/shard_map/ppermute | solution.py:42
  39.7 17.4 %collective-permute-start.9 = (f32[16,24,128]{2,1,0:T(8,128)S(1)}, f32[16,24,128]{2,1,0:T(8,128)S(1)}, u32[]{:S(2)}, u32[]{:S(2)}) collective-permute-start(f32[16,24,128]{2,1,0:T(8,128)S(1)} %add.123), channel_id=1, source_target_pairs={{0,4},{1,5},{2,6},{3,7},{8,12},{9,13},{10,14},{11,15},{16,20},{17,... | collective-permute-start | bytes 589832 | tf_op jit(solution)/shard_map/ppermute | solution.py:56
  42.4 32.7 %collective-permute-start.6 = (bf16[2,768,128]{2,1,0:T(8,128)(2,1)S(1)}, bf16[2,768,128]{2,1,0:T(8,128)(2,1)S(1)}, u32[]{:S(2)}, u32[]{:S(2)}) collective-permute-start(bf16[2,768,128]{2,1,0:T(8,128)(2,1)S(1)} %shard_map.118.rest_2_), channel_id=1, source_target_pairs={{0,1},{1,0},{2,3},{3,2},{4,5},{5,4},{6,7},{7,6},{8,9},{9,8},{10,11... | collective-permute-start | bytes 1179656 | tf_op jit(solution)/shard_map/ppermute | solution.py:37
  43.8 17.8 %collective-permute-start.16 = (bf16[768,128]{1,0:T(8,128)(2,1)}, bf16[768,128]{1,0:T(8,128)(2,1)}, u32[]{:S(2)}, u32[]{:S(2)}) collective-permute-start(bf16[768,128]{1,0:T(8,128)(2,1)} %get-tuple-element.62), channel_id=1, source_target_pairs={{0,6},{1,7},{2,4},{3,5},{4,2},{5,3},{6,0},{7,1},{8,14},{9,15},{10,... | collective-permute-start | bytes 589832 | tf_op jit(solution)/shard_map/ppermute | solution.py:32
  57.1 26.5 %collective-permute-start.15 = (bf16[2,768,128]{2,1,0:T(8,128)(2,1)S(1)}, bf16[2,768,128]{2,1,0:T(8,128)(2,1)S(1)}, u32[]{:S(2)}, u32[]{:S(2)}) collective-permute-start(bf16[2,768,128]{2,1,0:T(8,128)(2,1)S(1)} %collective-permute-done.12.rest_2_), channel_id=1, source_target_pairs={{0,1},{1,0},{2,3},{3,2},{4,5},{5,4},{6,7},{7,6},{8,9},{9,8},{10,11... | collective-permute-start | bytes 1179656 | tf_op jit(solution)/shard_map/ppermute | solution.py:37
  65.8 17.8 %collective-permute-start.13 = (bf16[768,128]{1,0:T(8,128)(2,1)}, bf16[768,128]{1,0:T(8,128)(2,1)S(1)}, u32[]{:S(2)}, u32[]{:S(2)}) collective-permute-start(bf16[768,128]{1,0:T(8,128)(2,1)} %copy-done.11), channel_id=1, source_target_pairs={{0,1},{1,0},{2,3},{3,2},{4,5},{5,4},{6,7},{7,6},{8,9},{9,8},{10,11... | collective-permute-start | bytes 589832 | tf_op jit(solution)/shard_map/ppermute | solution.py:37
  66.3 17.3 %collective-permute-start.14 = (bf16[768,128]{1,0:T(8,128)(2,1)}, bf16[768,128]{1,0:T(8,128)(2,1)S(1)}, u32[]{:S(2)}, u32[]{:S(2)}) collective-permute-start(bf16[768,128]{1,0:T(8,128)(2,1)} %copy-done.15), channel_id=1, source_target_pairs={{0,1},{1,0},{2,3},{3,2},{4,5},{5,4},{6,7},{7,6},{8,9},{9,8},{10,11... | collective-permute-start | bytes 589832 | tf_op jit(solution)/shard_map/ppermute | solution.py:37
  70.7 20.2 %collective-permute-start.19 = (bf16[768,128]{1,0:T(8,128)(2,1)S(1)}, bf16[768,128]{1,0:T(8,128)(2,1)S(1)}, u32[]{:S(2)}, u32[]{:S(2)}) collective-permute-start(bf16[768,128]{1,0:T(8,128)(2,1)S(1)} %shard_map.122), channel_id=1, source_target_pairs={{0,8},{8,16},{16,24},{1,9},{9,17},{17,25},{2,10},{10,18},{18,26},{... | collective-permute-start | bytes 589832 | tf_op jit(solution)/shard_map/ppermute | solution.py:47
  95.0 19.7 %collective-permute-start.22 = (bf16[768,128]{1,0:T(8,128)(2,1)S(1)}, bf16[768,128]{1,0:T(8,128)(2,1)S(1)}, u32[]{:S(2)}, u32[]{:S(2)}) collective-permute-start(bf16[768,128]{1,0:T(8,128)(2,1)S(1)} %get-tuple-element.65.u_ref.rest_0_), channel_id=1, source_target_pairs={{0,4},{1,5},{2,6},{3,7},{4,0},{5,1},{6,2},{7,3},{8,12},{9,13},{10,... | collective-permute-start | bytes 589832 | tf_op jit(solution)/shard_map/ppermute | solution.py:32
  99.8 17.6 %collective-permute-start.20 = (bf16[768,128]{1,0:T(8,128)(2,1)S(1)}, bf16[768,128]{1,0:T(8,128)(2,1)}, u32[]{:S(2)}, u32[]{:S(2)}) collective-permute-start(bf16[768,128]{1,0:T(8,128)(2,1)S(1)} %get-tuple-element.65.u_ref.rest_0_), channel_id=1, source_target_pairs={{0,2},{1,3},{2,0},{3,1},{4,6},{5,7},{6,4},{7,5},{8,10},{9,11},{10,... | collective-permute-start | bytes 589832 | tf_op jit(solution)/shard_map/ppermute | solution.py:32
  119.7 21.7 %collective-permute-start.29 = (bf16[2,768,128]{2,1,0:T(8,128)(2,1)S(1)}, bf16[2,768,128]{2,1,0:T(8,128)(2,1)S(1)}, u32[]{:S(2)}, u32[]{:S(2)}) collective-permute-start(bf16[2,768,128]{2,1,0:T(8,128)(2,1)S(1)} %shard_map.126.rest_2_), channel_id=1, source_target_pairs={{8,0},{16,8},{24,16},{9,1},{17,9},{25,17},{10,2},{18,10},{26,18},{... | collective-permute-start | bytes 1179656 | tf_op jit(solution)/shard_map/ppermute | solution.py:42
  123.7 17.2 %collective-permute-start.34 = (bf16[768,128]{1,0:T(8,128)(2,1)S(1)}, bf16[768,128]{1,0:T(8,128)(2,1)S(1)}, u32[]{:S(2)}, u32[]{:S(2)}) collective-permute-start(bf16[768,128]{1,0:T(8,128)(2,1)S(1)} %get-tuple-element.76), channel_id=1, source_target_pairs={{0,4},{1,5},{2,6},{3,7},{4,0},{5,1},{6,2},{7,3},{8,12},{9,13},{10,... | collective-permute-start | bytes 589832 | tf_op jit(solution)/shard_map/ppermute | solution.py:32
  128.7 20.5 %collective-permute-start.26 = (bf16[2,768,128]{2,1,0:T(8,128)(2,1)S(1)}, bf16[2,768,128]{2,1,0:T(8,128)(2,1)S(1)}, u32[]{:S(2)}, u32[]{:S(2)}) collective-permute-start(bf16[2,768,128]{2,1,0:T(8,128)(2,1)S(1)} %shard_map.126.rest_2_), channel_id=1, source_target_pairs={{0,1},{1,0},{2,3},{3,2},{4,5},{5,4},{6,7},{7,6},{8,9},{9,8},{10,11... | collective-permute-start | bytes 1179656 | tf_op jit(solution)/shard_map/ppermute | solution.py:37
  159.0 18.3 %collective-permute-start.38 = (bf16[4,768,128]{2,1,0:T(8,128)(2,1)S(1)}, bf16[4,768,128]{2,1,0:T(8,128)(2,1)S(1)}, u32[]{:S(2)}, u32[]{:S(2)}) collective-permute-start(bf16[4,768,128]{2,1,0:T(8,128)(2,1)S(1)} %get-tuple-element.81), channel_id=1, source_target_pairs={{0,1},{1,0},{2,3},{3,2},{4,5},{5,4},{6,7},{7,6},{8,9},{9,8},{10,11... | collective-permute-start | bytes 2359304 | tf_op jit(solution)/shard_map/ppermute | solution.py:37
  160.7 19.5 %collective-permute-start.39 = (bf16[768,128]{1,0:T(8,128)(2,1)S(1)}, bf16[768,128]{1,0:T(8,128)(2,1)S(1)}, u32[]{:S(2)}, u32[]{:S(2)}) collective-permute-start(bf16[768,128]{1,0:T(8,128)(2,1)S(1)} %get-tuple-element.79.u_ref.rest_0_), channel_id=1, source_target_pairs={{0,4},{1,5},{2,6},{3,7},{4,0},{5,1},{6,2},{7,3},{8,12},{9,13},{10,... | collective-permute-start | bytes 589832 | tf_op jit(solution)/shard_map/ppermute | solution.py:32
  166.2 17.9 %collective-permute-start.41 = (bf16[768,128]{1,0:T(8,128)(2,1)S(1)}, bf16[768,128]{1,0:T(8,128)(2,1)S(1)}, u32[]{:S(2)}, u32[]{:S(2)}) collective-permute-start(bf16[768,128]{1,0:T(8,128)(2,1)S(1)} %get-tuple-element.79.u_ref.rest_0_), channel_id=1, source_target_pairs={{0,1},{1,0},{2,3},{3,2},{4,5},{5,4},{6,7},{7,6},{8,9},{9,8},{10,11... | collective-permute-start | bytes 589832 | tf_op jit(solution)/shard_map/ppermute | solution.py:37
  180.9 21.8 %collective-permute-start.46 = (bf16[2,768,128]{2,1,0:T(8,128)(2,1)S(1)}, bf16[2,768,128]{2,1,0:T(8,128)(2,1)S(1)}, u32[]{:S(2)}, u32[]{:S(2)}) collective-permute-start(bf16[2,768,128]{2,1,0:T(8,128)(2,1)S(1)} %shard_map.134.rest_2_), channel_id=1, source_target_pairs={{8,0},{16,8},{24,16},{9,1},{17,9},{25,17},{10,2},{18,10},{26,18},{... | collective-permute-start | bytes 1179656 | tf_op jit(solution)/shard_map/ppermute | solution.py:42
  182.7 28.1 %collective-permute-start.43 = (bf16[2,768,128]{2,1,0:T(8,128)(2,1)S(1)}, bf16[2,768,128]{2,1,0:T(8,128)(2,1)S(1)}, u32[]{:S(2)}, u32[]{:S(2)}) collective-permute-start(bf16[2,768,128]{2,1,0:T(8,128)(2,1)S(1)} %shard_map.134.rest_2_), channel_id=1, source_target_pairs={{0,1},{1,0},{2,3},{3,2},{4,5},{5,4},{6,7},{7,6},{8,9},{9,8},{10,11... | collective-permute-start | bytes 1179656 | tf_op jit(solution)/shard_map/ppermute | solution.py:37
  224.9 26.5 %collective-permute-start.57 = (bf16[768,128]{1,0:T(8,128)(2,1)S(1)}, bf16[768,128]{1,0:T(8,128)(2,1)S(1)}, u32[]{:S(2)}, u32[]{:S(2)}) collective-permute-start(bf16[768,128]{1,0:T(8,128)(2,1)S(1)} %get-tuple-element.93.u_ref.rest_0_), channel_id=1, source_target_pairs={{0,6},{1,7},{2,4},{3,5},{4,2},{5,3},{6,0},{7,1},{8,14},{9,15},{10,... | collective-permute-start | bytes 589832 | tf_op jit(solution)/shard_map/ppermute | solution.py:32
  226.4 25.6 %collective-permute-start.54 = (bf16[768,128]{1,0:T(8,128)(2,1)S(1)}, bf16[768,128]{1,0:T(8,128)(2,1)S(1)}, u32[]{:S(2)}, u32[]{:S(2)}) collective-permute-start(bf16[768,128]{1,0:T(8,128)(2,1)S(1)} %get-tuple-element.93.u_ref.rest_0_), channel_id=1, source_target_pairs={{0,2},{1,3},{2,0},{3,1},{4,6},{5,7},{6,4},{7,5},{8,10},{9,11},{10,... | collective-permute-start | bytes 589832 | tf_op jit(solution)/shard_map/ppermute | solution.py:32
  227.0 26.2 %collective-permute-start.58 = (bf16[768,128]{1,0:T(8,128)(2,1)S(1)}, bf16[768,128]{1,0:T(8,128)(2,1)S(1)}, u32[]{:S(2)}, u32[]{:S(2)}) collective-permute-start(bf16[768,128]{1,0:T(8,128)(2,1)S(1)} %get-tuple-element.93.u_ref.rest_0_), channel_id=1, source_target_pairs={{0,1},{1,0},{2,3},{3,2},{4,5},{5,4},{6,7},{7,6},{8,9},{9,8},{10,11... | collective-permute-start | bytes 589832 | tf_op jit(solution)/shard_map/ppermute | solution.py:37
  229.3 26.3 %collective-permute-start.67 = (bf16[768,128]{1,0:T(8,128)(2,1)S(1)}, bf16[768,128]{1,0:T(8,128)(2,1)S(1)}, u32[]{:S(2)}, u32[]{:S(2)}) collective-permute-start(bf16[768,128]{1,0:T(8,128)(2,1)S(1)} %get-tuple-element.103), channel_id=1, source_target_pairs={{0,6},{1,7},{2,4},{3,5},{4,2},{5,3},{6,0},{7,1},{8,14},{9,15},{10,... | collective-permute-start | bytes 589832 | tf_op jit(solution)/shard_map/ppermute | solution.py:32
  237.2 21.1 %collective-permute-start.68 = (bf16[768,128]{1,0:T(8,128)(2,1)S(1)}, bf16[768,128]{1,0:T(8,128)(2,1)S(1)}, u32[]{:S(2)}, u32[]{:S(2)}) collective-permute-start(bf16[768,128]{1,0:T(8,128)(2,1)S(1)} %get-tuple-element.104), channel_id=1, source_target_pairs={{0,4},{1,5},{2,6},{3,7},{4,0},{5,1},{6,2},{7,3},{8,12},{9,13},{10,... | collective-permute-start | bytes 589832 | tf_op jit(solution)/shard_map/ppermute | solution.py:32
  258.3 17.2 %collective-permute-start.60 = (bf16[2,768,128]{2,1,0:T(8,128)(2,1)S(1)}, bf16[2,768,128]{2,1,0:T(8,128)(2,1)S(1)}, u32[]{:S(2)}, u32[]{:S(2)}) collective-permute-start(bf16[2,768,128]{2,1,0:T(8,128)(2,1)S(1)} %shard_map.142.rest_2_), channel_id=1, source_target_pairs={{0,1},{1,0},{2,3},{3,2},{4,5},{5,4},{6,7},{7,6},{8,9},{9,8},{10,11... | collective-permute-start | bytes 1179656 | tf_op jit(solution)/shard_map/ppermute | solution.py:37
  262.6 21.9 %collective-permute-start.64 = (bf16[768,128]{1,0:T(8,128)(2,1)}, bf16[768,128]{1,0:T(8,128)(2,1)}, u32[]{:S(2)}, u32[]{:S(2)}) collective-permute-start(bf16[768,128]{1,0:T(8,128)(2,1)} %collective-permute-done.61.rest_0_), channel_id=1, source_target_pairs={{0,1},{1,0},{2,3},{3,2},{4,5},{5,4},{6,7},{7,6},{8,9},{9,8},{10,11... | collective-permute-start | bytes 589832 | tf_op jit(solution)/shard_map/ppermute | solution.py:37
  265.7 18.8 %collective-permute-start.65 = (bf16[768,128]{1,0:T(8,128)(2,1)}, bf16[768,128]{1,0:T(8,128)(2,1)}, u32[]{:S(2)}, u32[]{:S(2)}) collective-permute-start(bf16[768,128]{1,0:T(8,128)(2,1)} %collective-permute-done.62.rest_1_), channel_id=1, source_target_pairs={{0,1},{1,0},{2,3},{3,2},{4,5},{5,4},{6,7},{7,6},{8,9},{9,8},{10,11... | collective-permute-start | bytes 589832 | tf_op jit(solution)/shard_map/ppermute | solution.py:37
  267.2 25.1 %collective-permute-start.70 = (bf16[768,128]{1,0:T(8,128)(2,1)}, bf16[768,128]{1,0:T(8,128)(2,1)}, u32[]{:S(2)}, u32[]{:S(2)}) collective-permute-start(bf16[768,128]{1,0:T(8,128)(2,1)} %shard_map.146), channel_id=1, source_target_pairs={{0,8},{8,16},{16,24},{1,9},{9,17},{17,25},{2,10},{10,18},{18,26},{... | collective-permute-start | bytes 589832 | tf_op jit(solution)/shard_map/ppermute | solution.py:47
  (96 other events, 1017.7 us)
where the time goes:
time: 299 us; the launch traced here: 294 us
  starting transfers between devices  102 us (34%)
  waiting for transfers between devices  78.1 us (26%)
  Pallas kernels  51.9 us (17%)
  local copies, waits for them, and re-layouts  35.2 us (12%)
  other arithmetic  25.4 us (8%)
    ppermute x24, waiting for transfers between devices, chip_swap(): return lax.ppermute(x, 'row', [(i, partner(i, by)) for i in range(total)])  54.8 us
    pallas_call x32, Pallas kernels, local_call(): pl.pallas_call(kernel, in_specs=in_specs, out_specs=[VMEM] * len(out_shap...  51.9 us
    ppermute x24, starting transfers between devices, chip_swap(): return lax.ppermute(x, 'row', [(i, partner(i, by)) for i in range(total)])  33.2 us
    unnamed x110, local copies, waits for them, and re-layouts  32.8 us
    ppermute x28, starting transfers between devices, core_swap(): return lax.ppermute(x, 'row', [(i, i ^ 1) for i in range(total)])  22.8 us
    ppermute x4, starting transfers between devices, to_block_above(): return lax.ppermute(x, 'sym', [(i, i + 1) for i in range(count - 1)])  21.6 us
    ppermute x12, starting transfers between devices, to_block_below(): return lax.ppermute(x, 'sym', [(i, i - 1) for i in range(1, count)])  15.6 us
    ppermute x12, waiting for transfers between devices, to_block_below(): return lax.ppermute(x, 'sym', [(i, i - 1) for i in range(1, count)])  13.8 us
  transfers between devices with their start and end apart: 73, of which 21 were waited for; matrix products, arithmetic and copies ran while one was open for 11% of the time, Pallas kernels for 15%

commit v1 on v0

--- a/solution.py
+++ b/solution.py
@@ -60,16 +60,21 @@
 
 VMEM = pl.BlockSpec(memory_space=pltpu.VMEM)
 SMEM = pl.BlockSpec(memory_space=pltpu.SMEM)
-
-
-def local_call(kernel, out_shape, in_specs, operands, flops=0, scratch=()):
+HBM = pl.BlockSpec(memory_space=pltpu.HBM)
+STREAM_GRANT = 47
+ROW_PARTS = 4
+SUB_COPIES = 6
+BLOCK_COPIES = 4
+
+
+def local_call(kernel, out_shape, in_specs, operands, flops=0, scratch=(), grant=7):
     return pl.pallas_call(
         kernel,
         in_specs=in_specs,
         out_specs=[VMEM] * len(out_shape),
         out_shape=out_shape,
         scratch_shapes=list(scratch),
-        compiler_params=pltpu.CompilerParams(vmem_limit_bytes=7 * 2**20),
+        compiler_params=pltpu.CompilerParams(vmem_limit_bytes=grant * 2**20),
         cost_estimate=pl.CostEstimate(flops=flops, bytes_accessed=0, transcendentals=0),
     )(*operands)
 
@@ -78,12 +83,51 @@
     return pl.ds(pl.multiple_of(index_ref[j] * rows, 128), rows)
 
 
-def give_kernel(index_ref, d_ref, u_ref, out_ref, ut_ref):
-    rows = u_ref.shape[0]
+def column_copies(index_ref, d_ref, held, sems, k):
+    rows = held.shape[1]
+    part = rows // BLOCK_COPIES
+    return [
+        pltpu.make_async_copy(
+            d_ref.at[pl.ds(i * part, part), columns_of(index_ref, k, rows)],
+            held.at[k, pl.ds(i * part, part)],
+            sems.at[k, i],
+        )
+        for i in range(BLOCK_COPIES)
+    ]
+
+
+def each(count, act):
+    def step(k, carry):
+        act(k)
+        return carry
+
+    lax.fori_loop(0, count, step, 0)
+
+
+def start_all(copies):
+    for copy in copies:
+        copy.start()
+
+
+def wait_all(copies):
+    for copy in copies:
+        copy.wait()
+
+
+def give_kernel(index_ref, d_ref, u_ref, out_ref, ut_ref, held, sems):
+    chips = held.shape[0]
+    each(chips, lambda k: start_all(column_copies(index_ref, d_ref, held, sems, k)))
     ut_ref[...] = u_ref[...].astype(F32).T.astype(BF16)
-    for k in range(out_ref.shape[0]):
-        part = dot(ut_ref[...], d_ref[:, columns_of(index_ref, k, rows)])
-        out_ref[k] = part.T.astype(BF16)
+
+    def block(k):
+        wait_all(column_copies(index_ref, d_ref, held, sems, k))
+        out_ref[k] = dot(ut_ref[...], held[k]).T.astype(BF16)
+
+    each(chips, block)
+
+
+def column_scratch(chips, rows):
+    return [pltpu.VMEM((chips, rows, rows), BF16), pltpu.SemaphoreType.DMA((chips, BLOCK_COPIES))]
 
 
 def lift_give(index, dipole_rows, u):
@@ -95,18 +139,22 @@
             jax.ShapeDtypeStruct((chips, rows, columns), BF16),
             jax.ShapeDtypeStruct((columns, rows), BF16),
         ],
-        [SMEM, VMEM, VMEM],
+        [SMEM, HBM, VMEM],
         [index, dipole_rows, u],
         flops=2 * rows * rows * chips * columns,
+        scratch=column_scratch(chips, rows),
+        grant=STREAM_GRANT,
     )
 
 
 def keep_kernel(index_ref, d_ref, ut_ref, carry_ref, *rest):
-    *outs, token = rest
-    rows = ut_ref.shape[1]
+    *outs, token, held, sems = rest
+    chips = held.shape[0]
+    each(chips, lambda k: start_all(column_copies(index_ref, d_ref, held, sems, k)))
     for k, out in enumerate(outs):
-        part = dot(ut_ref[...], d_ref[:, columns_of(index_ref, k, rows)])
-        out[...] = (part.T + carry_ref[k].astype(F32)).astype(BF16)
+        wait_all(column_copies(index_ref, d_ref, held, sems, k))
+        part = dot(ut_ref[...], held[k]).T
+        out[...] = (part + carry_ref[k].astype(F32)).astype(BF16)
     token[...] = jnp.zeros_like(token)
 
 
@@ -117,9 +165,11 @@
         keep_kernel,
         [jax.ShapeDtypeStruct((rows, columns), BF16)] * chips
         + [jax.ShapeDtypeStruct((8, 128), F32)],
-        [SMEM, VMEM, VMEM, VMEM],
+        [SMEM, HBM, VMEM, VMEM],
         [index, dipole_rows, ut, carry],
         flops=2 * rows * rows * chips * columns,
+        scratch=column_scratch(chips, rows),
+        grant=STREAM_GRANT,
     )
     return lifted, token
 
@@ -150,28 +200,50 @@
             j += 1
 
 
-def row_dots(out, matrix, whole, finish):
-    half = out.shape[0] // 2
-
-    def step(i, carry):
-        where = pl.ds(pl.multiple_of(i * half, 8), half)
-        finish(where, dot(matrix[where, :], whole[...]))
-        return carry
-
-    lax.fori_loop(0, 2, step, 0)
+def row_copies(matrix, held, sems, i):
+    part = held.shape[0] // ROW_PARTS
+    sub = part // SUB_COPIES
+    places = [pl.ds(pl.multiple_of(i * part + n * sub, sub), sub) for n in range(SUB_COPIES)]
+    return [
+        pltpu.make_async_copy(matrix.at[at], held.at[at], sems.at[i, n])
+        for n, at in enumerate(places)
+    ]
+
+
+def row_dots(matrix, held, sems, whole, prepare, finish):
+    part = held.shape[0] // ROW_PARTS
+    each(ROW_PARTS, lambda i: start_all(row_copies(matrix, held, sems, i)))
+    prepare()
+
+    def block(i):
+        wait_all(row_copies(matrix, held, sems, i))
+        where = pl.ds(pl.multiple_of(i * part, part), part)
+        finish(where, dot(held[where, :], whole[...]))
+
+    each(ROW_PARTS, block)
+
+
+def row_scratch(held, columns):
+    return [
+        pltpu.VMEM((held.shape[1], columns), BF16),
+        pltpu.VMEM(held.shape, BF16),
+        pltpu.SemaphoreType.DMA((ROW_PARTS, SUB_COPIES)),
+    ]
 
 
 def own_kernel(index_ref, h_ref, g_ref, *rest):
-    *refs, y_ref, ghost_ref, whole = rest
-    assemble(index_ref, whole, refs)
+    *refs, y_ref, ghost_ref, whole, held, sems = rest
+
+    def prepare():
+        assemble(index_ref, whole, refs)
+        ghosts = ghost_ref.shape[0]
+        ghost = dot(g_ref[...], whole[...])
+        ghost_ref[...] = ghost[:ghosts] + ghost[ghosts:]
 
     def finish(where, product):
         y_ref[where, :] = product
 
-    row_dots(y_ref, h_ref, whole, finish)
-    ghosts = ghost_ref.shape[0]
-    ghost = dot(g_ref[...], whole[...])
-    ghost_ref[...] = ghost[:ghosts] + ghost[ghosts:]
+    row_dots(h_ref, held, sems, whole, prepare, finish)
 
 
 def own_product(index, held, ghosts, refs):
@@ -183,10 +255,11 @@
             jax.ShapeDtypeStruct((rows, columns), F32),
             jax.ShapeDtypeStruct((ghosts.shape[0] // 2, columns), F32),
         ],
-        [SMEM] + [VMEM] * (2 + len(refs)),
+        [SMEM, HBM] + [VMEM] * (1 + len(refs)),
         [index, held, ghosts, *refs],
         flops=2 * held.shape[0] * states * columns,
-        scratch=[pltpu.VMEM((states, columns), BF16)],
+        scratch=row_scratch(held, columns),
+        grant=STREAM_GRANT,
     )
 
 
@@ -251,8 +324,7 @@
 def upper_kernel(
     index_ref, d_ref, y_ref, hot_ref, slope_ref, surface_ref, vectors_ref, *rest
 ):
-    *refs, out, whole = rest
-    assemble(index_ref, whole, refs)
+    *refs, out, whole, held, sems = rest
 
     def finish(where, product):
         source = dot(hot_ref[where, :], slope_ref[...])
@@ -262,7 +334,9 @@
             + surface_ref[where, :] * source
         )
 
-    row_dots(out, d_ref, whole, finish)
+    row_dots(
+        d_ref, held, sems, whole, lambda: assemble(index_ref, whole, refs), finish
+    )
 
 
 def upper_product(index, held, y, hot, slope, surface, vectors, refs):
@@ -272,10 +346,11 @@
     return local_call(
         upper_kernel,
         [jax.ShapeDtypeStruct((rows, columns), F32)],
-        [SMEM] + [VMEM] * (len(operands) - 1),
+        [SMEM, HBM] + [VMEM] * (len(operands) - 2),
         operands,
         flops=2 * rows * states * columns,
-        scratch=[pltpu.VMEM((states, columns), BF16)],
+        scratch=row_scratch(held, columns),
+        grant=STREAM_GRANT,
     )[0]
 
 

time: 299 us -> 307 us (1.027)
  Pallas kernels: 51.9 us -> 84 us
  local copies, waits for them, and re-layouts: 35.2 us -> 13.1 us
    pallas_call x32, Pallas kernels: 51.9 us -> 84 us  [local_call(): pl.pallas_call(kernel, in_specs=in_specs, out_specs=[VMEM] * len(out_shap...]
    unnamed x110 -> x80, local copies, waits for them, and re-layouts: 32.8 us -> 10.7 us
  transfers between devices with their start and end apart: 73 -> 73, of which waited for: 21 -> 20; matrix products, arithmetic and copies ran while one was open for 11% -> 11% of each run, Pallas kernels for 15% -> 23%
where the time goes in v1:
time: 307 us; the launch traced here: 302 us
  starting transfers between devices  99.3 us (32%)
  Pallas kernels  84 us (27%)
  waiting for transfers between devices  78.4 us (26%)
  other arithmetic  25.4 us (8%)
  local copies, waits for them, and re-layouts  13.1 us (4%)
    pallas_call x32, Pallas kernels, local_call(): pl.pallas_call(kernel, in_specs=in_specs, out_specs=[VMEM] * len(out_shap...  84 us
    ppermute x24, waiting for transfers between devices, chip_swap(): return lax.ppermute(x, 'row', [(i, partner(i, by)) for i in range(total)])  54.9 us
    ppermute x24, starting transfers between devices, chip_swap(): return lax.ppermute(x, 'row', [(i, partner(i, by)) for i in range(total)])  30.5 us
    ppermute x28, starting transfers between devices, core_swap(): return lax.ppermute(x, 'row', [(i, i ^ 1) for i in range(total)])  23.1 us
    ppermute x4, starting transfers between devices, to_block_above(): return lax.ppermute(x, 'sym', [(i, i + 1) for i in range(count - 1)])  21.5 us
    ppermute x12, starting transfers between devices, to_block_below(): return lax.ppermute(x, 'sym', [(i, i - 1) for i in range(1, count)])  15.6 us
    ppermute x12, waiting for transfers between devices, to_block_below(): return lax.ppermute(x, 'sym', [(i, i - 1) for i in range(1, count)])  14 us
    unnamed x80, local copies, waits for them, and re-layouts  10.7 us
  transfers between devices with their start and end apart: 73, of which 20 were waited for; matrix products, arithmetic and copies ran while one was open for 11% of the time, Pallas kernels for 23%

profile of v1, /device:TPU:9, one launch (start us, length us, event | category | flops | bytes accessed | tf_op | source)
XLA Modules:
  0.0 302.1 jit_solution(18169834416235270442)
XLA Ops:
  5.3 4.5 %shard_map.116 = (bf16[4,768,128]{2,1,0:T(8,128)(2,1)}, bf16[128,768]{1,0:T(8,128)(2,1)S(1)}) custom-call(s32[4]{0:T(128)S(1)} %add_subtract_fusion.index_ref, bf16[768,6144]{1,0:T(8,128)(2,1)} %bitcast.23, bf16[768,128]{1,0:T(8,128)(2,1)S(1)} %bitcast_convert_fusion.u_ref.rest_0_), custom_call_target="tpu_custom_call" | custom-call | flops 603979776 | tf_op jit(solution)/shard_map/pallas_call | solution.py:71
  24.3 4.4 %shard_map.117 = (bf16[768,128]{1,0:T(8,128)(2,1)S(1)}, bf16[768,128]{1,0:T(8,128)(2,1)}, bf16[768,128]{1,0:T(8,128)(2,1)}, bf16[768,128]{1,0:T(8,128)(2,1)}, f32[8,128]{1,0:T(8,128)S(1)}) custom-call(s32[4]{0:T(128)S(1)} %fusion.26.index_ref, bf16[768,6144]{1,0:T(8,128)(2,1)} %bitcast.24, bf16[128,768]{1,0:T(8,128)(2,1)S(1)} %get-tuple-element.55.ut_ref, ...), custom_call_target="tpu_custom_call" | custom-call | flops 603979776 | tf_op jit(solution)/shard_map/pallas_call | solution.py:71
  41.4 5.8 %collective-permute-done.11.rest_1_ = bf16[768,128]{1,0:T(8,128)(2,1)S(1)} collective-permute-done((bf16[768,128]{1,0:T(8,128)(2,1)S(1)}, bf16[768,128]{1,0:T(8,128)(2,1)S(1)}, u32[]{:S(2)}, u32[]{:S(2)}) %collective-permute-start.11) | collective-permute-done | bytes 196640 | tf_op jit(solution)/shard_map/ppermute | solution.py:42
  48.0 6.1 %collective-permute-done.9 = f32[16,24,128]{2,1,0:T(8,128)S(1)} collective-permute-done((f32[16,24,128]{2,1,0:T(8,128)S(1)}, f32[16,24,128]{2,1,0:T(8,128)S(1)}, u32[]{:S(2)}, u32[]{:S(2)}) %collective-permute-start.9) | collective-permute-done | bytes 196640 | tf_op jit(solution)/shard_map/ppermute | solution.py:56
  67.7 4.4 %collective-permute-start.19 = (bf16[768,128]{1,0:T(8,128)(2,1)S(1)}, bf16[768,128]{1,0:T(8,128)(2,1)S(1)}, u32[]{:S(2)}, u32[]{:S(2)}) collective-permute-start(bf16[768,128]{1,0:T(8,128)(2,1)S(1)} %shard_map.122), channel_id=1, source_target_pairs={{0,8},{8,16},{16,24},{1,9},{9,17},{17,25},{2,10},{10,18},{18,26},{... | collective-permute-start | bytes 589832 | tf_op jit(solution)/shard_map/ppermute | solution.py:47
  72.1 5.5 %shard_map.119 = (f32[768,128]{1,0:T(8,128)S(1)}, f32[48,128]{1,0:T(8,128)S(1)}) custom-call(s32[8]{0:T(128)S(1)} %pad_add_fusion.index_ref, bf16[768,6144]{1,0:T(8,128)(2,1)} %bitcast.35, bf16[96,6144]{1,0:T(8,128)(2,1)S(1)} %pad_maximum_fusion.1.g_ref, bf16[768,128]{1,0:T(8,128)(2,1)S(1)} %bitcast_convert_fusion.u_ref.rest_0_, ...), custom_call_target="tpu_custom_call" | custom-call | flops 1207959552 | tf_op jit(solution)/shard_map/pallas_call | solution.py:71
  78.6 5.6 %shard_map.121.image_ref = f32[768,128]{1,0:T(8,128)S(1)} custom-call(s32[8]{0:T(128)S(1)} %pad_add_fusion.index_ref, bf16[768,6144]{1,0:T(8,128)(2,1)} %bitcast.25, f32[768,128]{1,0:T(8,128)S(1)} %get-tuple-element.58.y_ref, bf16[768,128]{1,0:T(8,128)(2,1)S(1)} %and_convert_fusion.hot_ref, bf16[128,128]{1,0:T(8,128)(2,1)S(1)} %get-tuple-element.60.slope_ref, ...), custom_call_target="tpu_custom_call" | custom-call | flops 1207959552 | tf_op jit(solution)/shard_map/pallas_call | solution.py:71
  84.5 4.5 %shard_map.124 = (bf16[4,768,128]{2,1,0:T(8,128)(2,1)}, bf16[128,768]{1,0:T(8,128)(2,1)S(1)}) custom-call(s32[4]{0:T(128)S(1)} %copy-done.18, bf16[768,6144]{1,0:T(8,128)(2,1)} %bitcast.26, bf16[768,128]{1,0:T(8,128)(2,1)S(1)} %get-tuple-element.65.u_ref.rest_0_), custom_call_target="tpu_custom_call" | custom-call | flops 603979776 | tf_op jit(solution)/shard_map/pallas_call | solution.py:71
  90.3 4.9 %collective-permute-start.22 = (bf16[768,128]{1,0:T(8,128)(2,1)S(1)}, bf16[768,128]{1,0:T(8,128)(2,1)S(1)}, u32[]{:S(2)}, u32[]{:S(2)}) collective-permute-start(bf16[768,128]{1,0:T(8,128)(2,1)S(1)} %get-tuple-element.65.u_ref.rest_0_), channel_id=1, source_target_pairs={{0,4},{1,5},{2,6},{3,7},{4,0},{5,1},{6,2},{7,3},{8,12},{9,13},{10,... | collective-permute-start | bytes 589832 | tf_op jit(solution)/shard_map/ppermute | solution.py:32
  98.0 3.3 %collective-permute-start.71 = (f32[8,24,128]{2,1,0:T(8,128)}, f32[8,24,128]{2,1,0:T(8,128)}, u32[]{:S(2)}, u32[]{:S(2)}) collective-permute-start(f32[8,24,128]{2,1,0:T(8,128)} %get-tuple-element.120), channel_id=1, source_target_pairs={{0,1},{1,2},{2,3},{3,4},{4,5},{5,6},{6,7},{8,9},{9,10},{10,11},{11... | collective-permute-start | bytes 294920 | tf_op jit(solution)/shard_map/ppermute | solution.py:452
  104.9 3.7 %shard_map.125 = (bf16[768,128]{1,0:T(8,128)(2,1)S(1)}, bf16[768,128]{1,0:T(8,128)(2,1)S(1)}, bf16[768,128]{1,0:T(8,128)(2,1)S(1)}, bf16[768,128]{1,0:T(8,128)(2,1)S(1)}, f32[8,128]{1,0:T(8,128)S(1)}) custom-call(s32[4]{0:T(128)S(1)} %copy-done.21, bf16[768,6144]{1,0:T(8,128)(2,1)} %bitcast.27, bf16[128,768]{1,0:T(8,128)(2,1)S(1)} %copy-done.12, ...), custom_call_target="tpu_custom_call" | custom-call | flops 603979776 | tf_op jit(solution)/shard_map/pallas_call | solution.py:71
  120.7 3.6 %collective-permute-done.28.rest_1_ = bf16[768,128]{1,0:T(8,128)(2,1)S(1)} collective-permute-done((bf16[768,128]{1,0:T(8,128)(2,1)}, bf16[768,128]{1,0:T(8,128)(2,1)S(1)}, u32[]{:S(2)}, u32[]{:S(2)}) %collective-permute-start.28) | collective-permute-done | bytes 196640 | tf_op jit(solution)/shard_map/ppermute | solution.py:42
  127.1 3.7 %collective-permute-done.33.refs_1_ = bf16[768,128]{1,0:T(8,128)(2,1)S(1)} collective-permute-done((bf16[768,128]{1,0:T(8,128)(2,1)S(1)}, bf16[768,128]{1,0:T(8,128)(2,1)S(1)}, u32[]{:S(2)}, u32[]{:S(2)}) %collective-permute-start.33) | collective-permute-done | bytes 196640 | tf_op jit(solution)/shard_map/ppermute | solution.py:32
  131.4 3.6 %collective-permute-done.34.refs_2_ = bf16[768,128]{1,0:T(8,128)(2,1)S(1)} collective-permute-done((bf16[768,128]{1,0:T(8,128)(2,1)S(1)}, bf16[768,128]{1,0:T(8,128)(2,1)S(1)}, u32[]{:S(2)}, u32[]{:S(2)}) %collective-permute-start.34) | collective-permute-done | bytes 196640 | tf_op jit(solution)/shard_map/ppermute | solution.py:32
  137.3 5.8 %collective-permute-start.36 = (bf16[768,128]{1,0:T(8,128)(2,1)S(1)}, bf16[768,128]{1,0:T(8,128)(2,1)S(1)}, u32[]{:S(2)}, u32[]{:S(2)}) collective-permute-start(bf16[768,128]{1,0:T(8,128)(2,1)S(1)} %shard_map.130), channel_id=1, source_target_pairs={{0,8},{8,16},{16,24},{1,9},{9,17},{17,25},{2,10},{10,18},{18,26},{... | collective-permute-start | bytes 589832 | tf_op jit(solution)/shard_map/ppermute | solution.py:47
  143.2 5.9 %shard_map.127 = (f32[768,128]{1,0:T(8,128)S(1)}, f32[48,128]{1,0:T(8,128)S(1)}) custom-call(s32[8]{0:T(128)S(1)} %pad_add_fusion.index_ref, bf16[768,6144]{1,0:T(8,128)(2,1)} %bitcast.36, bf16[96,6144]{1,0:T(8,128)(2,1)S(1)} %pad_maximum_fusion.1.g_ref, bf16[768,128]{1,0:T(8,128)(2,1)S(1)} %get-tuple-element.65.u_ref.rest_0_, ...), custom_call_target="tpu_custom_call" | custom-call | flops 1207959552 | tf_op jit(solution)/shard_map/pallas_call | solution.py:71
  149.3 5.6 %shard_map.129.image_ref = f32[768,128]{1,0:T(8,128)S(1)} custom-call(s32[8]{0:T(128)S(1)} %pad_add_fusion.index_ref, bf16[768,6144]{1,0:T(8,128)(2,1)} %bitcast.28, f32[768,128]{1,0:T(8,128)S(1)} %get-tuple-element.69.y_ref, bf16[768,128]{1,0:T(8,128)(2,1)S(1)} %and_convert_fusion.hot_ref, bf16[128,128]{1,0:T(8,128)(2,1)S(1)} %get-tuple-element.73.slope_ref, ...), custom_call_target="tpu_custom_call" | custom-call | flops 1207959552 | tf_op jit(solution)/shard_map/pallas_call | solution.py:71
  155.1 3.6 %shard_map.132 = (bf16[4,768,128]{2,1,0:T(8,128)(2,1)S(1)}, bf16[128,768]{1,0:T(8,128)(2,1)S(1)}) custom-call(s32[4]{0:T(128)S(1)} %copy-done.19, bf16[768,6144]{1,0:T(8,128)(2,1)} %bitcast.29, bf16[768,128]{1,0:T(8,128)(2,1)S(1)} %get-tuple-element.79.u_ref.rest_0_), custom_call_target="tpu_custom_call" | custom-call | flops 603979776 | tf_op jit(solution)/shard_map/pallas_call | solution.py:71
  166.7 8.7 %collective-permute-done.37.rest_1_ = bf16[768,128]{1,0:T(8,128)(2,1)S(1)} collective-permute-done((bf16[768,128]{1,0:T(8,128)(2,1)S(1)}, bf16[768,128]{1,0:T(8,128)(2,1)S(1)}, u32[]{:S(2)}, u32[]{:S(2)}) %collective-permute-start.37) | collective-permute-done | bytes 196640 | tf_op jit(solution)/shard_map/ppermute | solution.py:32
  178.0 3.7 %shard_map.133 = (bf16[768,128]{1,0:T(8,128)(2,1)S(1)}, bf16[768,128]{1,0:T(8,128)(2,1)S(1)}, bf16[768,128]{1,0:T(8,128)(2,1)S(1)}, bf16[768,128]{1,0:T(8,128)(2,1)S(1)}, f32[8,128]{1,0:T(8,128)S(1)}) custom-call(s32[4]{0:T(128)S(1)} %copy-done.22, bf16[768,6144]{1,0:T(8,128)(2,1)} %bitcast.30, bf16[128,768]{1,0:T(8,128)(2,1)S(1)} %get-tuple-element.80.ut_ref, ...), custom_call_target="tpu_custom_call" | custom-call | flops 603979776 | tf_op jit(solution)/shard_map/pallas_call | solution.py:71
  191.0 9.4 %collective-permute-done.50.refs_1_ = bf16[768,128]{1,0:T(8,128)(2,1)S(1)} collective-permute-done((bf16[768,128]{1,0:T(8,128)(2,1)S(1)}, bf16[768,128]{1,0:T(8,128)(2,1)S(1)}, u32[]{:S(2)}, u32[]{:S(2)}) %collective-permute-start.50) | collective-permute-done | bytes 196640 | tf_op jit(solution)/shard_map/ppermute | solution.py:32
  206.3 6.4 %collective-permute-start.53 = (bf16[768,128]{1,0:T(8,128)(2,1)S(1)}, bf16[768,128]{1,0:T(8,128)(2,1)S(1)}, u32[]{:S(2)}, u32[]{:S(2)}) collective-permute-start(bf16[768,128]{1,0:T(8,128)(2,1)S(1)} %shard_map.138), channel_id=1, source_target_pairs={{0,8},{8,16},{16,24},{1,9},{9,17},{17,25},{2,10},{10,18},{18,26},{... | collective-permute-start | bytes 589832 | tf_op jit(solution)/shard_map/ppermute | solution.py:47
  212.7 5.5 %shard_map.135 = (f32[768,128]{1,0:T(8,128)S(1)}, f32[48,128]{1,0:T(8,128)S(1)}) custom-call(s32[8]{0:T(128)S(1)} %pad_add_fusion.index_ref, bf16[768,6144]{1,0:T(8,128)(2,1)} %bitcast.37, bf16[96,6144]{1,0:T(8,128)(2,1)S(1)} %pad_maximum_fusion.1.g_ref, bf16[768,128]{1,0:T(8,128)(2,1)S(1)} %get-tuple-element.79.u_ref.rest_0_, ...), custom_call_target="tpu_custom_call" | custom-call | flops 1207959552 | tf_op jit(solution)/shard_map/pallas_call | solution.py:71
  218.4 5.6 %shard_map.137.image_ref = f32[768,128]{1,0:T(8,128)S(1)} custom-call(s32[8]{0:T(128)S(1)} %pad_add_fusion.index_ref, bf16[768,6144]{1,0:T(8,128)(2,1)} %bitcast.31, f32[768,128]{1,0:T(8,128)S(1)} %get-tuple-element.83.y_ref, bf16[768,128]{1,0:T(8,128)(2,1)S(1)} %and_convert_fusion.hot_ref, bf16[128,128]{1,0:T(8,128)(2,1)S(1)} %get-tuple-element.87.slope_ref, ...), custom_call_target="tpu_custom_call" | custom-call | flops 1207959552 | tf_op jit(solution)/shard_map/pallas_call | solution.py:71
  224.2 3.6 %shard_map.140 = (bf16[4,768,128]{2,1,0:T(8,128)(2,1)S(1)}, bf16[128,768]{1,0:T(8,128)(2,1)S(1)}) custom-call(s32[4]{0:T(128)S(1)} %copy-done.19, bf16[768,6144]{1,0:T(8,128)(2,1)} %bitcast.32, bf16[768,128]{1,0:T(8,128)(2,1)S(1)} %get-tuple-element.93.u_ref.rest_0_), custom_call_target="tpu_custom_call" | custom-call | flops 603979776 | tf_op jit(solution)/shard_map/pallas_call | solution.py:71
  235.5 3.7 %shard_map.141 = (bf16[768,128]{1,0:T(8,128)(2,1)S(1)}, bf16[768,128]{1,0:T(8,128)(2,1)S(1)}, bf16[768,128]{1,0:T(8,128)(2,1)S(1)}, bf16[768,128]{1,0:T(8,128)(2,1)S(1)}, f32[8,128]{1,0:T(8,128)S(1)}) custom-call(s32[4]{0:T(128)S(1)} %copy-done.22, bf16[768,6144]{1,0:T(8,128)(2,1)} %bitcast.33, bf16[128,768]{1,0:T(8,128)(2,1)S(1)} %get-tuple-element.94.ut_ref, ...), custom_call_target="tpu_custom_call" | custom-call | flops 603979776 | tf_op jit(solution)/shard_map/pallas_call | solution.py:71
  239.6 5.0 %collective-permute-done.56.refs_0_ = bf16[768,128]{1,0:T(8,128)(2,1)S(1)} collective-permute-done((bf16[768,128]{1,0:T(8,128)(2,1)S(1)}, bf16[768,128]{1,0:T(8,128)(2,1)S(1)}, u32[]{:S(2)}, u32[]{:S(2)}) %collective-permute-start.56) | collective-permute-done | bytes 196640 | tf_op jit(solution)/shard_map/ppermute | solution.py:32
  244.6 3.4 %collective-permute-start.68 = (bf16[768,128]{1,0:T(8,128)(2,1)S(1)}, bf16[768,128]{1,0:T(8,128)(2,1)S(1)}, u32[]{:S(2)}, u32[]{:S(2)}) collective-permute-start(bf16[768,128]{1,0:T(8,128)(2,1)S(1)} %get-tuple-element.104), channel_id=1, source_target_pairs={{0,4},{1,5},{2,6},{3,7},{4,0},{5,1},{6,2},{7,3},{8,12},{9,13},{10,... | collective-permute-start | bytes 589832 | tf_op jit(solution)/shard_map/ppermute | solution.py:32
  247.9 11.2 %collective-permute-done.57.refs_1_ = bf16[768,128]{1,0:T(8,128)(2,1)S(1)} collective-permute-done((bf16[768,128]{1,0:T(8,128)(2,1)S(1)}, bf16[768,128]{1,0:T(8,128)(2,1)S(1)}, u32[]{:S(2)}, u32[]{:S(2)}) %collective-permute-start.57) | collective-permute-done | bytes 196640 | tf_op jit(solution)/shard_map/ppermute | solution.py:32
  275.0 4.9 %collective-permute-start.70 = (bf16[768,128]{1,0:T(8,128)(2,1)}, bf16[768,128]{1,0:T(8,128)(2,1)}, u32[]{:S(2)}, u32[]{:S(2)}) collective-permute-start(bf16[768,128]{1,0:T(8,128)(2,1)} %shard_map.146), channel_id=1, source_target_pairs={{0,8},{8,16},{16,24},{1,9},{9,17},{17,25},{2,10},{10,18},{18,26},{... | collective-permute-start | bytes 589832 | tf_op jit(solution)/shard_map/ppermute | solution.py:47
  283.3 5.5 %shard_map.143 = (f32[768,128]{1,0:T(8,128)S(1)}, f32[48,128]{1,0:T(8,128)S(1)}) custom-call(s32[8]{0:T(128)S(1)} %pad_add_fusion.index_ref, bf16[768,6144]{1,0:T(8,128)(2,1)} %bitcast.38, bf16[96,6144]{1,0:T(8,128)(2,1)S(1)} %pad_maximum_fusion.1.g_ref, bf16[768,128]{1,0:T(8,128)(2,1)S(1)} %get-tuple-element.93.u_ref.rest_0_, ...), custom_call_target="tpu_custom_call" | custom-call | flops 1207959552 | tf_op jit(solution)/shard_map/pallas_call | solution.py:71
  293.9 6.3 %shard_map.145.image_ref = f32[768,128]{1,0:T(8,128)S(1)} custom-call(s32[8]{0:T(128)S(1)} %pad_add_fusion.index_ref, bf16[768,6144]{1,0:T(8,128)(2,1)} %bitcast.34, f32[768,128]{1,0:T(8,128)S(1)} %get-tuple-element.97.y_ref, bf16[768,128]{1,0:T(8,128)(2,1)S(1)} %and_convert_fusion.hot_ref, bf16[128,128]{1,0:T(8,128)(2,1)S(1)} %get-tuple-element.101.slope_ref, ...), custom_call_target="tpu_custom_call" | custom-call | flops 1207959552 | tf_op jit(solution)/shard_map/pallas_call | solution.py:71
  (286 shorter events, 132.7 us)
Async XLA Ops:
  1.7 27.1 %collective-permute-start.2 = (bf16[768,128]{1,0:T(8,128)(2,1)S(1)}, bf16[768,128]{1,0:T(8,128)(2,1)S(1)}, u32[]{:S(2)}, u32[]{:S(2)}) collective-permute-start(bf16[768,128]{1,0:T(8,128)(2,1)S(1)} %bitcast_convert_fusion.u_ref.rest_0_), channel_id=1, source_target_pairs={{0,4},{1,5},{2,6},{3,7},{4,0},{5,1},{6,2},{7,3},{8,12},{9,13},{10,... | collective-permute-start | bytes 589832 | tf_op jit(solution)/shard_map/ppermute | solution.py:32
  4.0 26.1 %collective-permute-start.3 = (bf16[768,128]{1,0:T(8,128)(2,1)S(1)}, bf16[768,128]{1,0:T(8,128)(2,1)S(1)}, u32[]{:S(2)}, u32[]{:S(2)}) collective-permute-start(bf16[768,128]{1,0:T(8,128)(2,1)S(1)} %bitcast_convert_fusion.u_ref.rest_0_), channel_id=1, source_target_pairs={{0,6},{1,7},{2,4},{3,5},{4,2},{5,3},{6,0},{7,1},{8,14},{9,15},{10,... | collective-permute-start | bytes 589832 | tf_op jit(solution)/shard_map/ppermute | solution.py:32
  4.0 28.1 %collective-permute-start = (bf16[768,128]{1,0:T(8,128)(2,1)S(1)}, bf16[768,128]{1,0:T(8,128)(2,1)S(1)}, u32[]{:S(2)}, u32[]{:S(2)}) collective-permute-start(bf16[768,128]{1,0:T(8,128)(2,1)S(1)} %bitcast_convert_fusion.u_ref.rest_0_), channel_id=1, source_target_pairs={{0,2},{1,3},{2,0},{3,1},{4,6},{5,7},{6,4},{7,5},{8,10},{9,11},{10,... | collective-permute-start | bytes 589832 | tf_op jit(solution)/shard_map/ppermute | solution.py:32
  23.0 17.7 %collective-permute-start.10 = (bf16[768,128]{1,0:T(8,128)(2,1)S(1)}, bf16[768,128]{1,0:T(8,128)(2,1)S(1)}, u32[]{:S(2)}, u32[]{:S(2)}) collective-permute-start(bf16[768,128]{1,0:T(8,128)(2,1)S(1)} %bitcast_convert_fusion.u_ref.rest_0_), channel_id=1, source_target_pairs={{8,0},{16,8},{24,16},{9,1},{17,9},{25,17},{10,2},{18,10},{26,18},{... | collective-permute-start | bytes 589832 | tf_op jit(solution)/shard_map/ppermute | solution.py:42
  30.1 24.0 %collective-permute-start.12 = (bf16[2,768,128]{2,1,0:T(8,128)(2,1)S(1)}, bf16[2,768,128]{2,1,0:T(8,128)(2,1)S(1)}, u32[]{:S(2)}, u32[]{:S(2)}) collective-permute-start(bf16[2,768,128]{2,1,0:T(8,128)(2,1)S(1)} %shard_map.118.rest_2_), channel_id=1, source_target_pairs={{8,0},{16,8},{24,16},{9,1},{17,9},{25,17},{10,2},{18,10},{26,18},{... | collective-permute-start | bytes 1179656 | tf_op jit(solution)/shard_map/ppermute | solution.py:42
  36.7 17.4 %collective-permute-start.9 = (f32[16,24,128]{2,1,0:T(8,128)S(1)}, f32[16,24,128]{2,1,0:T(8,128)S(1)}, u32[]{:S(2)}, u32[]{:S(2)}) collective-permute-start(f32[16,24,128]{2,1,0:T(8,128)S(1)} %add.123), channel_id=1, source_target_pairs={{0,4},{1,5},{2,6},{3,7},{8,12},{9,13},{10,14},{11,15},{16,20},{17,... | collective-permute-start | bytes 589832 | tf_op jit(solution)/shard_map/ppermute | solution.py:56
  39.4 32.7 %collective-permute-start.6 = (bf16[2,768,128]{2,1,0:T(8,128)(2,1)S(1)}, bf16[2,768,128]{2,1,0:T(8,128)(2,1)S(1)}, u32[]{:S(2)}, u32[]{:S(2)}) collective-permute-start(bf16[2,768,128]{2,1,0:T(8,128)(2,1)S(1)} %shard_map.118.rest_2_), channel_id=1, source_target_pairs={{0,1},{1,0},{2,3},{3,2},{4,5},{5,4},{6,7},{7,6},{8,9},{9,8},{10,11... | collective-permute-start | bytes 1179656 | tf_op jit(solution)/shard_map/ppermute | solution.py:37
  40.7 17.8 %collective-permute-start.16 = (bf16[768,128]{1,0:T(8,128)(2,1)}, bf16[768,128]{1,0:T(8,128)(2,1)}, u32[]{:S(2)}, u32[]{:S(2)}) collective-permute-start(bf16[768,128]{1,0:T(8,128)(2,1)} %get-tuple-element.62), channel_id=1, source_target_pairs={{0,6},{1,7},{2,4},{3,5},{4,2},{5,3},{6,0},{7,1},{8,14},{9,15},{10,... | collective-permute-start | bytes 589832 | tf_op jit(solution)/shard_map/ppermute | solution.py:32
  54.1 24.5 %collective-permute-start.15 = (bf16[2,768,128]{2,1,0:T(8,128)(2,1)S(1)}, bf16[2,768,128]{2,1,0:T(8,128)(2,1)S(1)}, u32[]{:S(2)}, u32[]{:S(2)}) collective-permute-start(bf16[2,768,128]{2,1,0:T(8,128)(2,1)S(1)} %collective-permute-done.12.rest_2_), channel_id=1, source_target_pairs={{0,1},{1,0},{2,3},{3,2},{4,5},{5,4},{6,7},{7,6},{8,9},{9,8},{10,11... | collective-permute-start | bytes 1179656 | tf_op jit(solution)/shard_map/ppermute | solution.py:37
  90.3 18.3 %collective-permute-start.22 = (bf16[768,128]{1,0:T(8,128)(2,1)S(1)}, bf16[768,128]{1,0:T(8,128)(2,1)S(1)}, u32[]{:S(2)}, u32[]{:S(2)}) collective-permute-start(bf16[768,128]{1,0:T(8,128)(2,1)S(1)} %get-tuple-element.65.u_ref.rest_0_), channel_id=1, source_target_pairs={{0,4},{1,5},{2,6},{3,7},{4,0},{5,1},{6,2},{7,3},{8,12},{9,13},{10,... | collective-permute-start | bytes 589832 | tf_op jit(solution)/shard_map/ppermute | solution.py:32
  95.2 17.6 %collective-permute-start.20 = (bf16[768,128]{1,0:T(8,128)(2,1)S(1)}, bf16[768,128]{1,0:T(8,128)(2,1)}, u32[]{:S(2)}, u32[]{:S(2)}) collective-permute-start(bf16[768,128]{1,0:T(8,128)(2,1)S(1)} %get-tuple-element.65.u_ref.rest_0_), channel_id=1, source_target_pairs={{0,2},{1,3},{2,0},{3,1},{4,6},{5,7},{6,4},{7,5},{8,10},{9,11},{10,... | collective-permute-start | bytes 589832 | tf_op jit(solution)/shard_map/ppermute | solution.py:32
  98.0 17.1 %collective-permute-start.71 = (f32[8,24,128]{2,1,0:T(8,128)}, f32[8,24,128]{2,1,0:T(8,128)}, u32[]{:S(2)}, u32[]{:S(2)}) collective-permute-start(f32[8,24,128]{2,1,0:T(8,128)} %get-tuple-element.120), channel_id=1, source_target_pairs={{0,1},{1,2},{2,3},{3,4},{4,5},{5,6},{6,7},{8,9},{9,10},{10,11},{11... | collective-permute-start | bytes 294920 | tf_op jit(solution)/shard_map/ppermute | solution.py:452
  115.1 20.4 %collective-permute-start.29 = (bf16[2,768,128]{2,1,0:T(8,128)(2,1)S(1)}, bf16[2,768,128]{2,1,0:T(8,128)(2,1)S(1)}, u32[]{:S(2)}, u32[]{:S(2)}) collective-permute-start(bf16[2,768,128]{2,1,0:T(8,128)(2,1)S(1)} %shard_map.126.rest_2_), channel_id=1, source_target_pairs={{8,0},{16,8},{24,16},{9,1},{17,9},{25,17},{10,2},{18,10},{26,18},{... | collective-permute-start | bytes 1179656 | tf_op jit(solution)/shard_map/ppermute | solution.py:42
  124.3 18.9 %collective-permute-start.26 = (bf16[2,768,128]{2,1,0:T(8,128)(2,1)S(1)}, bf16[2,768,128]{2,1,0:T(8,128)(2,1)S(1)}, u32[]{:S(2)}, u32[]{:S(2)}) collective-permute-start(bf16[2,768,128]{2,1,0:T(8,128)(2,1)S(1)} %shard_map.126.rest_2_), channel_id=1, source_target_pairs={{0,1},{1,0},{2,3},{3,2},{4,5},{5,4},{6,7},{7,6},{8,9},{9,8},{10,11... | collective-permute-start | bytes 1179656 | tf_op jit(solution)/shard_map/ppermute | solution.py:37
  137.3 17.6 %collective-permute-start.36 = (bf16[768,128]{1,0:T(8,128)(2,1)S(1)}, bf16[768,128]{1,0:T(8,128)(2,1)S(1)}, u32[]{:S(2)}, u32[]{:S(2)}) collective-permute-start(bf16[768,128]{1,0:T(8,128)(2,1)S(1)} %shard_map.130), channel_id=1, source_target_pairs={{0,8},{8,16},{16,24},{1,9},{9,17},{17,25},{2,10},{10,18},{18,26},{... | collective-permute-start | bytes 589832 | tf_op jit(solution)/shard_map/ppermute | solution.py:47
  158.7 18.0 %collective-permute-start.38 = (bf16[4,768,128]{2,1,0:T(8,128)(2,1)S(1)}, bf16[4,768,128]{2,1,0:T(8,128)(2,1)S(1)}, u32[]{:S(2)}, u32[]{:S(2)}) collective-permute-start(bf16[4,768,128]{2,1,0:T(8,128)(2,1)S(1)} %get-tuple-element.81), channel_id=1, source_target_pairs={{0,1},{1,0},{2,3},{3,2},{4,5},{5,4},{6,7},{7,6},{8,9},{9,8},{10,11... | collective-permute-start | bytes 2359304 | tf_op jit(solution)/shard_map/ppermute | solution.py:37
  160.4 21.4 %collective-permute-start.39 = (bf16[768,128]{1,0:T(8,128)(2,1)S(1)}, bf16[768,128]{1,0:T(8,128)(2,1)S(1)}, u32[]{:S(2)}, u32[]{:S(2)}) collective-permute-start(bf16[768,128]{1,0:T(8,128)(2,1)S(1)} %get-tuple-element.79.u_ref.rest_0_), channel_id=1, source_target_pairs={{0,4},{1,5},{2,6},{3,7},{4,0},{5,1},{6,2},{7,3},{8,12},{9,13},{10,... | collective-permute-start | bytes 589832 | tf_op jit(solution)/shard_map/ppermute | solution.py:32
  163.5 18.2 %collective-permute-start.40 = (bf16[768,128]{1,0:T(8,128)(2,1)S(1)}, bf16[768,128]{1,0:T(8,128)(2,1)S(1)}, u32[]{:S(2)}, u32[]{:S(2)}) collective-permute-start(bf16[768,128]{1,0:T(8,128)(2,1)S(1)} %get-tuple-element.79.u_ref.rest_0_), channel_id=1, source_target_pairs={{0,6},{1,7},{2,4},{3,5},{4,2},{5,3},{6,0},{7,1},{8,14},{9,15},{10,... | collective-permute-start | bytes 589832 | tf_op jit(solution)/shard_map/ppermute | solution.py:32
  165.9 19.7 %collective-permute-start.41 = (bf16[768,128]{1,0:T(8,128)(2,1)S(1)}, bf16[768,128]{1,0:T(8,128)(2,1)S(1)}, u32[]{:S(2)}, u32[]{:S(2)}) collective-permute-start(bf16[768,128]{1,0:T(8,128)(2,1)S(1)} %get-tuple-element.79.u_ref.rest_0_), channel_id=1, source_target_pairs={{0,1},{1,0},{2,3},{3,2},{4,5},{5,4},{6,7},{7,6},{8,9},{9,8},{10,11... | collective-permute-start | bytes 589832 | tf_op jit(solution)/shard_map/ppermute | solution.py:37
  181.8 22.8 %collective-permute-start.46 = (bf16[2,768,128]{2,1,0:T(8,128)(2,1)S(1)}, bf16[2,768,128]{2,1,0:T(8,128)(2,1)S(1)}, u32[]{:S(2)}, u32[]{:S(2)}) collective-permute-start(bf16[2,768,128]{2,1,0:T(8,128)(2,1)S(1)} %shard_map.134.rest_2_), channel_id=1, source_target_pairs={{8,0},{16,8},{24,16},{9,1},{17,9},{25,17},{10,2},{18,10},{26,18},{... | collective-permute-start | bytes 1179656 | tf_op jit(solution)/shard_map/ppermute | solution.py:42
  183.7 29.1 %collective-permute-start.43 = (bf16[2,768,128]{2,1,0:T(8,128)(2,1)S(1)}, bf16[2,768,128]{2,1,0:T(8,128)(2,1)S(1)}, u32[]{:S(2)}, u32[]{:S(2)}) collective-permute-start(bf16[2,768,128]{2,1,0:T(8,128)(2,1)S(1)} %shard_map.134.rest_2_), channel_id=1, source_target_pairs={{0,1},{1,0},{2,3},{3,2},{4,5},{5,4},{6,7},{7,6},{8,9},{9,8},{10,11... | collective-permute-start | bytes 1179656 | tf_op jit(solution)/shard_map/ppermute | solution.py:37
  186.8 16.8 %collective-permute-start.51 = (bf16[768,128]{1,0:T(8,128)(2,1)S(1)}, bf16[768,128]{1,0:T(8,128)(2,1)S(1)}, u32[]{:S(2)}, u32[]{:S(2)}) collective-permute-start(bf16[768,128]{1,0:T(8,128)(2,1)S(1)} %get-tuple-element.90), channel_id=1, source_target_pairs={{0,4},{1,5},{2,6},{3,7},{4,0},{5,1},{6,2},{7,3},{8,12},{9,13},{10,... | collective-permute-start | bytes 589832 | tf_op jit(solution)/shard_map/ppermute | solution.py:32
  206.3 17.7 %collective-permute-start.53 = (bf16[768,128]{1,0:T(8,128)(2,1)S(1)}, bf16[768,128]{1,0:T(8,128)(2,1)S(1)}, u32[]{:S(2)}, u32[]{:S(2)}) collective-permute-start(bf16[768,128]{1,0:T(8,128)(2,1)S(1)} %shard_map.138), channel_id=1, source_target_pairs={{0,8},{8,16},{16,24},{1,9},{9,17},{17,25},{2,10},{10,18},{18,26},{... | collective-permute-start | bytes 589832 | tf_op jit(solution)/shard_map/ppermute | solution.py:47
  232.6 26.5 %collective-permute-start.57 = (bf16[768,128]{1,0:T(8,128)(2,1)S(1)}, bf16[768,128]{1,0:T(8,128)(2,1)S(1)}, u32[]{:S(2)}, u32[]{:S(2)}) collective-permute-start(bf16[768,128]{1,0:T(8,128)(2,1)S(1)} %get-tuple-element.93.u_ref.rest_0_), channel_id=1, source_target_pairs={{0,6},{1,7},{2,4},{3,5},{4,2},{5,3},{6,0},{7,1},{8,14},{9,15},{10,... | collective-permute-start | bytes 589832 | tf_op jit(solution)/shard_map/ppermute | solution.py:32
  233.7 26.0 %collective-permute-start.54 = (bf16[768,128]{1,0:T(8,128)(2,1)S(1)}, bf16[768,128]{1,0:T(8,128)(2,1)S(1)}, u32[]{:S(2)}, u32[]{:S(2)}) collective-permute-start(bf16[768,128]{1,0:T(8,128)(2,1)S(1)} %get-tuple-element.93.u_ref.rest_0_), channel_id=1, source_target_pairs={{0,2},{1,3},{2,0},{3,1},{4,6},{5,7},{6,4},{7,5},{8,10},{9,11},{10,... | collective-permute-start | bytes 589832 | tf_op jit(solution)/shard_map/ppermute | solution.py:32
  234.8 26.3 %collective-permute-start.58 = (bf16[768,128]{1,0:T(8,128)(2,1)S(1)}, bf16[768,128]{1,0:T(8,128)(2,1)S(1)}, u32[]{:S(2)}, u32[]{:S(2)}) collective-permute-start(bf16[768,128]{1,0:T(8,128)(2,1)S(1)} %get-tuple-element.93.u_ref.rest_0_), channel_id=1, source_target_pairs={{0,1},{1,0},{2,3},{3,2},{4,5},{5,4},{6,7},{7,6},{8,9},{9,8},{10,11... | collective-permute-start | bytes 589832 | tf_op jit(solution)/shard_map/ppermute | solution.py:37
  239.2 24.1 %collective-permute-start.67 = (bf16[768,128]{1,0:T(8,128)(2,1)S(1)}, bf16[768,128]{1,0:T(8,128)(2,1)S(1)}, u32[]{:S(2)}, u32[]{:S(2)}) collective-permute-start(bf16[768,128]{1,0:T(8,128)(2,1)S(1)} %get-tuple-element.103), channel_id=1, source_target_pairs={{0,6},{1,7},{2,4},{3,5},{4,2},{5,3},{6,0},{7,1},{8,14},{9,15},{10,... | collective-permute-start | bytes 589832 | tf_op jit(solution)/shard_map/ppermute | solution.py:32
  244.6 21.1 %collective-permute-start.68 = (bf16[768,128]{1,0:T(8,128)(2,1)S(1)}, bf16[768,128]{1,0:T(8,128)(2,1)S(1)}, u32[]{:S(2)}, u32[]{:S(2)}) collective-permute-start(bf16[768,128]{1,0:T(8,128)(2,1)S(1)} %get-tuple-element.104), channel_id=1, source_target_pairs={{0,4},{1,5},{2,6},{3,7},{4,0},{5,1},{6,2},{7,3},{8,12},{9,13},{10,... | collective-permute-start | bytes 589832 | tf_op jit(solution)/shard_map/ppermute | solution.py:32
  265.7 17.6 %collective-permute-start.60 = (bf16[2,768,128]{2,1,0:T(8,128)(2,1)S(1)}, bf16[2,768,128]{2,1,0:T(8,128)(2,1)S(1)}, u32[]{:S(2)}, u32[]{:S(2)}) collective-permute-start(bf16[2,768,128]{2,1,0:T(8,128)(2,1)S(1)} %shard_map.142.rest_2_), channel_id=1, source_target_pairs={{0,1},{1,0},{2,3},{3,2},{4,5},{5,4},{6,7},{7,6},{8,9},{9,8},{10,11... | collective-permute-start | bytes 1179656 | tf_op jit(solution)/shard_map/ppermute | solution.py:37
  270.4 23.5 %collective-permute-start.64 = (bf16[768,128]{1,0:T(8,128)(2,1)}, bf16[768,128]{1,0:T(8,128)(2,1)}, u32[]{:S(2)}, u32[]{:S(2)}) collective-permute-start(bf16[768,128]{1,0:T(8,128)(2,1)} %collective-permute-done.61.rest_0_), channel_id=1, source_target_pairs={{0,1},{1,0},{2,3},{3,2},{4,5},{5,4},{6,7},{7,6},{8,9},{9,8},{10,11... | collective-permute-start | bytes 589832 | tf_op jit(solution)/shard_map/ppermute | solution.py:37
  273.4 20.5 %collective-permute-start.65 = (bf16[768,128]{1,0:T(8,128)(2,1)}, bf16[768,128]{1,0:T(8,128)(2,1)}, u32[]{:S(2)}, u32[]{:S(2)}) collective-permute-start(bf16[768,128]{1,0:T(8,128)(2,1)} %collective-permute-done.62.rest_1_), channel_id=1, source_target_pairs={{0,1},{1,0},{2,3},{3,2},{4,5},{5,4},{6,7},{7,6},{8,9},{9,8},{10,11... | collective-permute-start | bytes 589832 | tf_op jit(solution)/shard_map/ppermute | solution.py:37
  275.0 25.2 %collective-permute-start.70 = (bf16[768,128]{1,0:T(8,128)(2,1)}, bf16[768,128]{1,0:T(8,128)(2,1)}, u32[]{:S(2)}, u32[]{:S(2)}) collective-permute-start(bf16[768,128]{1,0:T(8,128)(2,1)} %shard_map.146), channel_id=1, source_target_pairs={{0,8},{8,16},{16,24},{1,9},{9,17},{17,25},{2,10},{10,18},{18,26},{... | collective-permute-start | bytes 589832 | tf_op jit(solution)/shard_map/ppermute | solution.py:47
  (81 other events, 885.6 us)
